TPU v7x, 32 devices: a whole 2x2x4 slice. The times are simulated.
32 devices in a mesh: dp: 4 (over y, x), shard: 8 (over z, core).
Axes of the slice: x: 2, y: 2, z: 4, core: 2. Of those that a mesh axis runs over, the one named last changes fastest.
Arguments:
- text_input: bfloat16 [4096, 768], P(('dp', 'shard')), may hold values from -6 to 6
- layout_input: bfloat16 [4096, 192], P(('dp', 'shard')), may hold values from -6 to 6
- text_cot: bfloat16 [4096, 768], P(('dp', 'shard')), may hold values from -6 to 6
- layout_cot: bfloat16 [4096, 192], P(('dp', 'shard')), may hold values from -6 to 6
- segment_ids: int32 [4096], P(('dp', 'shard')), may hold values from 0 to 63, as said below
- page_groups: int32 [64], P(('dp', 'shard')), may hold values from 0 to 7
- lang_table: bfloat16 [2, 6144], P(None, ('dp', 'shard')), may hold values from -3 to 3
- text_attn: bfloat16 [2, 768, 3072], P(None, None, ('dp', 'shard'))
- text_up: bfloat16 [2, 768, 3072], P(None, None, ('dp', 'shard')), may hold values from -0.21875 to 0.21875
- text_down: bfloat16 [2, 3072, 768], P(None, ('dp', 'shard')), may hold values from -0.109375 to 0.109375
- text_vector: bfloat16 [2, 9216], P(None, ('dp', 'shard'))
- layout_attn: bfloat16 [2, 192, 768], P(None, None, ('dp', 'shard'))
- layout_up: bfloat16 [2, 192, 768], P(None, None, ('dp', 'shard')), may hold values from -0.4375 to 0.4375
- layout_down: bfloat16 [2, 768, 192], P(None, ('dp', 'shard')), may hold values from -0.21875 to 0.21875
- layout_vector: bfloat16 [2, 2304], P(None, ('dp', 'shard'))
Outputs:
- text_out: float32 [4096, 768], P(('dp', 'shard'))
- layout_out: float32 [4096, 192], P(('dp', 'shard'))
- text_input_grad: float32 [4096, 768], P(('dp', 'shard'))
- layout_input_grad: float32 [4096, 192], P(('dp', 'shard'))
- text_attn_grad: float32 [2, 768, 3072], P(None, None, ('dp', 'shard'))
- text_up_grad: float32 [2, 768, 3072], P(None, None, ('dp', 'shard'))
- text_down_grad: float32 [2, 3072, 768], P(None, ('dp', 'shard'))
- text_vector_grad: float32 [2, 9216], P(None, ('dp', 'shard'))
- lang_table_grad: float32 [2, 6144], P(None, ('dp', 'shard'))
- layout_attn_grad: float32 [2, 192, 768], P(None, None, ('dp', 'shard'))
- layout_up_grad: float32 [2, 192, 768], P(None, None, ('dp', 'shard'))
- layout_down_grad: float32 [2, 768, 192], P(None, ('dp', 'shard'))
- layout_vector_grad: float32 [2, 2304], P(None, ('dp', 'shard'))
Inputs may be any that keep to these rules, and one draw needn't show every extreme that they name: `segment_ids`: each aligned block of 128 tokens (the tokens of one device) holds one or two whole pages, numbered 2b and 2b + 1 in block b, page 2b first; no page crosses a block; the first block is a single page of 128 tokens and the last block holds two pages.
All inputs are finite; a program needn't handle non-finite values.
Results may differ from a plain program's by a relative error of at most 0.025.
The roundings to bfloat16 on the way count: a program that leaves them out, or rounds other values in their place, can miss the bound.
Values may be sent and summed in bfloat16 or wider, within the bound.
A program may use at most 256 MiB of HBM per device.

v0:
```python
import functools
import math
from types import SimpleNamespace

import jax
import jax.numpy as jnp
from jax import lax
from jax.experimental import pallas as pl
from jax.experimental.pallas import tpu as pltpu
from jax.sharding import PartitionSpec as P

H = 12
LANGS = 8


EPSILON = 1e-05
MASKED = -1e30


def norm_rows(residual, norm_gain, norm_shift):
    average = jnp.mean(residual, axis=-1, keepdims=True)
    centred = residual - average
    variance = jnp.mean(centred * centred, axis=-1, keepdims=True)
    return centred * lax.rsqrt(variance + EPSILON) * norm_gain + norm_shift


def exact_gelu(values):
    return jax.nn.gelu(values, approximate=False)


def norm_back(residual, norm_gain, norm_shift, grad_rows):
    unused, pullback = jax.vjp(norm_rows, residual, norm_gain, norm_shift)
    return pullback(grad_rows)


def gelu_back(upper, grad_rows):
    unused, pullback = jax.vjp(exact_gelu, upper)
    return pullback(grad_rows)[0]


def column_sum(matrix):
    return jnp.sum(matrix.astype(jnp.float32), axis=0)


def unpack(vector, stream_width, hidden_width):
    values = vector.astype(jnp.float32)
    pieces = [values[member * stream_width : (member + 1) * stream_width] for member in range(8)]
    return pieces + [values[8 * stream_width : 8 * stream_width + hidden_width]]


def project(stream_low, attn_weight, pieces):
    stream_width = stream_low.shape[1]
    joined = jnp.dot(
        stream_low, attn_weight[:, : 3 * stream_width], preferred_element_type=jnp.float32
    )
    head_shape = (stream_low.shape[0], H, stream_width // H)
    query = (joined[:, :stream_width] + pieces[0]).astype(jnp.bfloat16).reshape(head_shape)
    keyed = joined[:, stream_width : 2 * stream_width].astype(jnp.bfloat16).reshape(head_shape)
    valued = (joined[:, 2 * stream_width :] + pieces[1]).astype(jnp.bfloat16).reshape(head_shape)
    return (query, keyed, valued)


def joint_scores(text_heads, layout_heads, same_page):
    text_part = jnp.einsum(
        "shd,thd->hst", text_heads[0], text_heads[1], preferred_element_type=jnp.float32
    )
    layout_part = jnp.einsum(
        "shd,thd->hst", layout_heads[0], layout_heads[1], preferred_element_type=jnp.float32
    )
    combined = text_part * (1.0 / math.sqrt(text_heads[0].shape[2])) + layout_part * (
        1.0 / math.sqrt(layout_heads[0].shape[2])
    )
    return jnp.where(same_page[None], combined, MASKED)


def attend(probs_low, valued):
    context = jnp.einsum("hst,thd->shd", probs_low, valued, preferred_element_type=jnp.float32)
    return context.reshape(context.shape[0], -1).astype(jnp.bfloat16)


def tail_forward(stream_rows, context_low, attn_weight, up_weight, down_weight, pieces):
    stream_width = stream_rows.shape[1]
    branch = (
        jnp.dot(context_low, attn_weight[:, 3 * stream_width :], preferred_element_type=jnp.float32)
        + pieces[2]
    )
    first_sum = stream_rows + branch
    normed = norm_rows(first_sum, pieces[4], pieces[5])
    normed_low = normed.astype(jnp.bfloat16)
    upper = jnp.dot(normed_low, up_weight, preferred_element_type=jnp.float32) + pieces[8]
    active_low = exact_gelu(upper).astype(jnp.bfloat16)
    second_sum = (
        normed + jnp.dot(active_low, down_weight, preferred_element_type=jnp.float32) + pieces[3]
    )
    result = norm_rows(second_sum, pieces[6], pieces[7])
    return (result, (first_sum, normed_low, upper, active_low, second_sum))


def layer_forward(text_rows, layout_rows, text_weights, layout_weights, same_page, onehot):
    group_table = text_weights[4].astype(jnp.float32).reshape(onehot.shape[1], -1)
    text_rows = text_rows + jnp.dot(onehot, group_table, precision=lax.Precision.HIGHEST)
    text_pieces = unpack(text_weights[3], text_rows.shape[1], text_weights[1].shape[1])
    layout_pieces = unpack(layout_weights[3], layout_rows.shape[1], layout_weights[1].shape[1])
    text_low = text_rows.astype(jnp.bfloat16)
    layout_low = layout_rows.astype(jnp.bfloat16)
    text_heads = project(text_low, text_weights[0], text_pieces)
    layout_heads = project(layout_low, layout_weights[0], layout_pieces)
    scores = joint_scores(text_heads, layout_heads, same_page)
    row_peak = jnp.max(scores, axis=-1, keepdims=True)
    log_total = row_peak + jnp.log(jnp.sum(jnp.exp(scores - row_peak), axis=-1, keepdims=True))
    probs_low = jnp.exp(scores - log_total).astype(jnp.bfloat16)
    text_context = attend(probs_low, text_heads[2])
    layout_context = attend(probs_low, layout_heads[2])
    text_next, text_stored = tail_forward(
        text_rows, text_context, text_weights[0], text_weights[1], text_weights[2], text_pieces
    )
    layout_next, layout_stored = tail_forward(
        layout_rows,
        layout_context,
        layout_weights[0],
        layout_weights[1],
        layout_weights[2],
        layout_pieces,
    )
    stored = (
        text_low,
        layout_low,
        text_heads,
        layout_heads,
        log_total,
        text_context,
        layout_context,
        text_stored,
        layout_stored,
    )
    return (text_next, layout_next, stored)


def tail_backward(grad_result, stored, context_low, attn_weight, up_weight, down_weight, pieces):
    first_sum, normed_low, upper, active_low, second_sum = stored
    stream_width = first_sum.shape[1]
    grad_second, grad_gain_two, grad_shift_two = norm_back(
        second_sum, pieces[6], pieces[7], grad_result
    )
    grad_down_low = grad_second.astype(jnp.bfloat16)
    grad_down_bias = column_sum(grad_down_low)
    grad_down = jnp.einsum(
        "sf,sd->fd", active_low, grad_down_low, preferred_element_type=jnp.float32
    )
    grad_active = jnp.einsum(
        "sd,fd->sf", grad_down_low, down_weight, preferred_element_type=jnp.float32
    )
    grad_upper_low = gelu_back(upper, grad_active).astype(jnp.bfloat16)
    grad_up_bias = column_sum(grad_upper_low)
    grad_up = jnp.einsum(
        "sd,sf->df", normed_low, grad_upper_low, preferred_element_type=jnp.float32
    )
    grad_normed = grad_second + jnp.einsum(
        "sf,df->sd", grad_upper_low, up_weight, preferred_element_type=jnp.float32
    )
    grad_first, grad_gain_one, grad_shift_one = norm_back(
        first_sum, pieces[4], pieces[5], grad_normed
    )
    grad_branch_low = grad_first.astype(jnp.bfloat16)
    grad_out_bias = column_sum(grad_branch_low)
    output_weight = attn_weight[:, 3 * stream_width :]
    grad_output_proj = jnp.einsum(
        "sd,se->de", context_low, grad_branch_low, preferred_element_type=jnp.float32
    )
    grad_context = jnp.einsum(
        "se,de->sd", grad_branch_low, output_weight, preferred_element_type=jnp.float32
    ).astype(jnp.bfloat16)
    matrices = (grad_output_proj, grad_up, grad_down)
    vectors = (
        grad_out_bias,
        grad_down_bias,
        grad_gain_one,
        grad_shift_one,
        grad_gain_two,
        grad_shift_two,
        grad_up_bias,
    )
    return (grad_first, grad_context, matrices, vectors)


def head_grads(head_set, grad_context_low, probs_low, grad_scores_low):
    inverse_root = 1.0 / math.sqrt(head_set[0].shape[2])
    grad_heads = grad_context_low.reshape(head_set[2].shape)
    grad_query = (
        jnp.einsum("hst,thd->shd", grad_scores_low, head_set[1], preferred_element_type=jnp.float32)
        * inverse_root
    )
    grad_key = (
        jnp.einsum("hst,shd->thd", grad_scores_low, head_set[0], preferred_element_type=jnp.float32)
        * inverse_root
    )
    grad_value = jnp.einsum(
        "hst,shd->thd", probs_low, grad_heads, preferred_element_type=jnp.float32
    )
    row_count = head_set[0].shape[0]
    joined = jnp.concatenate(
        [
            grad_query.reshape(row_count, -1),
            grad_key.reshape(row_count, -1),
            grad_value.reshape(row_count, -1),
        ],
        axis=1,
    )
    return joined.astype(jnp.bfloat16)


def attention_backward(
    text_heads, layout_heads, log_total, same_page, grad_text_context, grad_layout_context
):
    scores = joint_scores(text_heads, layout_heads, same_page)
    probs = jnp.exp(scores - log_total)
    probs_low = probs.astype(jnp.bfloat16)
    grad_text_heads = grad_text_context.reshape(text_heads[2].shape)
    grad_layout_heads = grad_layout_context.reshape(layout_heads[2].shape)
    grad_probs = jnp.einsum(
        "shd,thd->hst", grad_text_heads, text_heads[2], preferred_element_type=jnp.float32
    )
    grad_probs = grad_probs + jnp.einsum(
        "shd,thd->hst", grad_layout_heads, layout_heads[2], preferred_element_type=jnp.float32
    )
    inner = jnp.sum(grad_probs * probs, axis=-1, keepdims=True)
    grad_scores_low = (probs * (grad_probs - inner)).astype(jnp.bfloat16)
    text_joined = head_grads(text_heads, grad_text_context, probs_low, grad_scores_low)
    layout_joined = head_grads(layout_heads, grad_layout_context, probs_low, grad_scores_low)
    return (text_joined, layout_joined)


def head_backward(stream_low, grad_joined_low, attn_weight, grad_first, matrices, vectors):
    stream_width = stream_low.shape[1]
    grad_in_proj = jnp.einsum(
        "sd,se->de", stream_low, grad_joined_low, preferred_element_type=jnp.float32
    )
    grad_bias_query = column_sum(grad_joined_low[:, :stream_width])
    grad_bias_value = column_sum(grad_joined_low[:, 2 * stream_width :])
    grad_stream = grad_first + jnp.einsum(
        "se,de->sd",
        grad_joined_low,
        attn_weight[:, : 3 * stream_width],
        preferred_element_type=jnp.float32,
    )
    grad_attn = jnp.concatenate([grad_in_proj, matrices[0]], axis=1)
    grad_vector = jnp.concatenate([grad_bias_query, grad_bias_value] + list(vectors))
    return (grad_stream, (grad_attn, matrices[1], matrices[2], grad_vector))


def layer_backward(grad_text, grad_layout, stored, text_weights, layout_weights, same_page, onehot):
    (
        text_low,
        layout_low,
        text_heads,
        layout_heads,
        log_total,
        text_context,
        layout_context,
        text_stored,
        layout_stored,
    ) = stored
    text_pieces = unpack(text_weights[3], text_low.shape[1], text_weights[1].shape[1])
    layout_pieces = unpack(layout_weights[3], layout_low.shape[1], layout_weights[1].shape[1])
    text_first, grad_text_context, text_mats, text_vecs = tail_backward(
        grad_text,
        text_stored,
        text_context,
        text_weights[0],
        text_weights[1],
        text_weights[2],
        text_pieces,
    )
    layout_first, grad_layout_context, layout_mats, layout_vecs = tail_backward(
        grad_layout,
        layout_stored,
        layout_context,
        layout_weights[0],
        layout_weights[1],
        layout_weights[2],
        layout_pieces,
    )
    text_joined, layout_joined = attention_backward(
        text_heads, layout_heads, log_total, same_page, grad_text_context, grad_layout_context
    )
    grad_text_in, text_terms = head_backward(
        text_low, text_joined, text_weights[0], text_first, text_mats, text_vecs
    )
    grad_layout_in, layout_terms = head_backward(
        layout_low, layout_joined, layout_weights[0], layout_first, layout_mats, layout_vecs
    )
    grad_group = jnp.einsum(
        "sg,sd->gd", onehot, grad_text_in, precision=lax.Precision.HIGHEST
    ).reshape(-1)
    return (grad_text_in, grad_layout_in, text_terms + (grad_group,), layout_terms)


def fetch_layer(
    text_attn,
    text_up,
    text_down,
    text_vector,
    lang_table,
    layout_attn,
    layout_up,
    layout_down,
    layout_vector,
    layer_index,
):
    fetched = (
        lax.all_gather(text_attn[layer_index], AXES, axis=1, tiled=True),
        lax.all_gather(text_up[layer_index], AXES, axis=1, tiled=True),
        lax.all_gather(text_down[layer_index], AXES, axis=0, tiled=True),
        lax.all_gather(text_vector[layer_index], AXES, axis=0, tiled=True),
        lax.all_gather(lang_table[layer_index], AXES, axis=0, tiled=True),
        lax.all_gather(layout_attn[layer_index], AXES, axis=1, tiled=True),
        lax.all_gather(layout_up[layer_index], AXES, axis=1, tiled=True),
        lax.all_gather(layout_down[layer_index], AXES, axis=0, tiled=True),
        lax.all_gather(layout_vector[layer_index], AXES, axis=0, tiled=True),
    )
    return (fetched[:5], fetched[5:])


def fetch_layer_back(
    text_attn,
    text_up,
    text_down,
    text_vector,
    lang_table,
    layout_attn,
    layout_up,
    layout_down,
    layout_vector,
    layer_index,
):
    fetched = (
        lax.all_gather(text_attn[layer_index], AXES, axis=1, tiled=True),
        lax.all_gather(text_up[layer_index], AXES, axis=1, tiled=True),
        lax.all_gather(text_down[layer_index], AXES, axis=0, tiled=True),
        lax.all_gather(text_vector[layer_index], AXES, axis=0, tiled=True),
        lax.all_gather(lang_table[layer_index], AXES, axis=0, tiled=True),
        lax.all_gather(layout_attn[layer_index], AXES, axis=1, tiled=True),
        lax.all_gather(layout_up[layer_index], AXES, axis=1, tiled=True),
        lax.all_gather(layout_down[layer_index], AXES, axis=0, tiled=True),
        lax.all_gather(layout_vector[layer_index], AXES, axis=0, tiled=True),
    )
    return (fetched[:5], fetched[5:])


def generic_shards(
    text_input,
    layout_input,
    text_cot,
    layout_cot,
    segment_ids,
    page_groups,
    lang_table,
    text_attn,
    text_up,
    text_down,
    text_vector,
    layout_attn,
    layout_up,
    layout_down,
    layout_vector,
):
    layer_count = text_attn.shape[0]
    same_page = segment_ids[:, None] == segment_ids[None, :]
    page_slot = segment_ids % 2
    token_group = jnp.where(page_slot == 0, page_groups[0], page_groups[1])
    onehot = (token_group[:, None] == jnp.arange(LANGS, dtype=jnp.int32)[None, :]).astype(
        jnp.float32
    )
    text_rows = text_input.astype(jnp.float32)
    layout_rows = layout_input.astype(jnp.float32)
    saved_layers = []
    for layer_index in range(layer_count):
        text_fetched, layout_fetched = fetch_layer(
            text_attn,
            text_up,
            text_down,
            text_vector,
            lang_table,
            layout_attn,
            layout_up,
            layout_down,
            layout_vector,
            layer_index,
        )
        text_rows, layout_rows, stored = layer_forward(
            text_rows, layout_rows, text_fetched, layout_fetched, same_page, onehot
        )
        saved_layers.append(stored)
    grad_text = text_cot.astype(jnp.float32)
    grad_layout = layout_cot.astype(jnp.float32)
    owned_all = [None] * layer_count
    for layer_index in reversed(range(layer_count)):
        text_fetched, layout_fetched = fetch_layer_back(
            text_attn,
            text_up,
            text_down,
            text_vector,
            lang_table,
            layout_attn,
            layout_up,
            layout_down,
            layout_vector,
            layer_index,
        )
        grad_text, grad_layout, text_terms, layout_terms = layer_backward(
            grad_text,
            grad_layout,
            saved_layers[layer_index],
            text_fetched,
            layout_fetched,
            same_page,
            onehot,
        )
        joined_terms = tuple(text_terms) + tuple(layout_terms)
        owned_all[layer_index] = (
            lax.psum_scatter(joined_terms[0], AXES, scatter_dimension=1, tiled=True),
            lax.psum_scatter(joined_terms[1], AXES, scatter_dimension=1, tiled=True),
            lax.psum_scatter(joined_terms[2], AXES, scatter_dimension=0, tiled=True),
            lax.psum_scatter(joined_terms[3], AXES, scatter_dimension=0, tiled=True),
            lax.psum_scatter(joined_terms[4], AXES, scatter_dimension=0, tiled=True),
            lax.psum_scatter(joined_terms[5], AXES, scatter_dimension=1, tiled=True),
            lax.psum_scatter(joined_terms[6], AXES, scatter_dimension=1, tiled=True),
            lax.psum_scatter(joined_terms[7], AXES, scatter_dimension=0, tiled=True),
            lax.psum_scatter(joined_terms[8], AXES, scatter_dimension=0, tiled=True),
        )
    stacks = [jnp.stack([owned[member] for owned in owned_all]) for member in range(9)]
    return (
        text_rows,
        layout_rows,
        grad_text,
        grad_layout,
        stacks[0],
        stacks[1],
        stacks[2],
        stacks[3],
        stacks[4],
        stacks[5],
        stacks[6],
        stacks[7],
        stacks[8],
    )


MESH = pl.DeviceIdType.MESH
AXES = ("dp", "shard")
ANY = pl.BlockSpec(memory_space=pl.ANY)
IN_VMEM = pl.BlockSpec(memory_space=pltpu.VMEM)
PLANE = 4
SUBLANES = 8
VECTOR_ROWS = 32


def fits_blocks(mesh):
    return mesh.shape[AXES[0]] == PLANE and mesh.shape[AXES[1]] == 2 * PLANE


def place(depth):
    dp, shard = lax.axis_index(AXES[0]), lax.axis_index(AXES[1])
    core, level = lax.rem(shard, 2), shard // 2
    dx = dp + 1 - 2 * lax.rem(dp, 2)
    dy = lax.rem(dp + 2, PLANE)
    me = dp * (2 * depth) + shard
    at = SimpleNamespace(dp=dp, z=level, core=core, dx=dx, dy=dy, dd=PLANE - 1 - dp, me=me)

    def device(plane_index, shard_index):
        return dict(zip(AXES, (plane_index, shard_index)))

    devices = SimpleNamespace(
        x=device(dx, shard),
        y=device(dy, shard),
        up=device(dp, lax.rem(shard + 2, 2 * depth)),
        down=device(dp, lax.rem(shard + 2 * depth - 2, 2 * depth)),
        far=device(dp, lax.rem(shard + depth, 2 * depth)),
        pair=device(dp, 2 * (level + 1 - 2 * lax.rem(level, 2)) + core),
        core=device(dp, shard + 1 - 2 * core),
    )
    return at, devices


def signal(devices):
    barrier = pltpu.get_barrier_semaphore()
    partners = (devices.x, devices.y, devices.up, devices.down, devices.far, devices.core)
    for partner in partners:
        pl.semaphore_signal(barrier, inc=1, device_id=partner, device_id_type=MESH)


def greeted():
    pl.semaphore_wait(pltpu.get_barrier_semaphore(), 6)


def remote(source, target, send_sem, recv_sem, device):
    return pltpu.make_async_remote_copy(
        src_ref=source,
        dst_ref=target,
        send_sem=send_sem,
        recv_sem=recv_sem,
        device_id=device,
        device_id_type=MESH,
    )


class AllSum:
    STEPS = 5

    def __init__(self, devices, running, held, landed, send_sem, recv_sem):
        self.partners = (devices.core, devices.pair, devices.far, devices.x, devices.y)
        self.running, self.held, self.landed = running, held, landed
        self.send_sem, self.recv_sem = send_sem, recv_sem

    def copy(self, step):
        return remote(
            self.held.at[step],
            self.landed.at[step],
            self.send_sem.at[step],
            self.recv_sem.at[step],
            self.partners[step],
        )

    def send(self, step):
        self.held[step] = self.running[...].astype(self.held.dtype)
        self.copy(step).start()

    def advance(self, step):
        self.copy(step).wait_recv()
        self.running[...] += self.landed[step].astype(jnp.float32)
        if step + 1 < self.STEPS:
            self.send(step + 1)

    def close(self):
        for step in range(self.STEPS):
            self.copy(step).wait_send()

    @classmethod
    def scratch(cls, shape):
        return [
            pltpu.VMEM((cls.STEPS,) + shape, jnp.bfloat16),
            pltpu.VMEM((cls.STEPS,) + shape, jnp.bfloat16),
            pltpu.SemaphoreType.DMA((cls.STEPS,)),
            pltpu.SemaphoreType.DMA((cls.STEPS,)),
        ]


class Plan:
    LAG = dict(x=1.8, z=1.8, c=1.0, h=0.3)
    PATIENCE = 1.0

    def __init__(self):
        self.tasks = []

    def add(self, name, run, after=(), needs=(), sends=(), time=0.2, rank=0, patient=False):
        self.tasks.append((name, run, tuple(after), tuple(needs), tuple(sends), time, rank, patient))

    def order(self):
        now, free, landed, done = 0.0, {}, {}, set()
        waiting, result = list(self.tasks), []
        while waiting:
            best = None
            for place_in_list, task in enumerate(waiting):
                name, run, after, needs, sends, time, rank, patient = task
                if any(other not in done for other in after):
                    continue
                if any(event not in landed for event in needs):
                    continue
                start = max([now] + [landed[event] for event in needs])
                key = (start + (self.PATIENCE if patient else 0.0), rank, place_in_list)
                if best is None or key < best[0]:
                    best = (key, task, start)
            assert best is not None
            task, start = best[1:]
            waiting.remove(task)
            result.append(task)
            name, run, after, needs, sends, time, rank, patient = task
            now = start + time
            done.add(name)
            for link, amount, event in sends:
                free[link] = max(now, free.get(link, 0.0)) + amount
                landed[event] = free[link] + self.LAG[link[0]]
        return result

    def run(self):
        for task in self.order():
            task[1]()


UNIT_ROWS_PER_US = 96 / 3.26


def add_rows(target, term):
    total = target[...].astype(jnp.float32) + term[...].astype(jnp.float32)
    target[...] = total.astype(target.dtype)


def add_units(target, *terms):
    def body(index, carry):
        total = target[index].astype(jnp.float32)
        for term in terms:
            total = total + term[index].astype(jnp.float32)
        target[index] = total.astype(target.dtype)
        return carry

    lax.fori_loop(0, target.shape[0], body, 0)


LANE = 128
PAD = 256
PIECE_ROWS = 12
TABLE_ROW = 12
SMALL_ROW = 20
SMALL_HIDDEN_ROW = 28


def dot_nt(left, right):
    return lax.dot_general(
        left, right, (((1,), (1,)), ((), ())), preferred_element_type=jnp.float32
    )


def dot_nn(left, right):
    return jnp.dot(left, right, preferred_element_type=jnp.float32)


def lane_of(shape):
    return lax.broadcasted_iota(jnp.int32, shape, len(shape) - 1)


def unit_rows(ref, dp):
    block = ref[dp]
    return block.reshape(-1, block.shape[-1])


def standard(residual, width):
    padded = residual.shape[1] != width
    average = jnp.sum(residual, axis=1, keepdims=True) * (1.0 / width)
    centred = residual - average
    if padded:
        centred = jnp.where(lane_of(residual.shape) < width, centred, 0.0)
    variance = jnp.sum(centred * centred, axis=1, keepdims=True) * (1.0 / width)
    scale = lax.rsqrt(variance + EPSILON)
    return centred * scale, scale


def gelu_parts(upper):
    cdf = 0.5 * (1.0 + lax.erf(upper * math.sqrt(0.5)))
    density = jnp.exp(upper * upper * -0.5) * (1.0 / math.sqrt(2.0 * math.pi))
    return upper * cdf, cdf + upper * density


def natural_rows(span, step):
    row = lax.broadcasted_iota(jnp.int32, (PAD, PAD), 0)
    column = lax.broadcasted_iota(jnp.int32, (PAD, PAD), 1)
    unit = jnp.zeros((PAD, PAD), jnp.int32)
    for n in range(1, PAD // step):
        unit = unit + jnp.where(row >= n * span, 1, 0)
    source = unit * step + row - unit * span
    return jnp.where((source == column) & (row < (PAD // step) * span), 1.0, 0.0)


def saved_shapes(layers, tokens, width, narrow_hidden):
    low, full = jnp.bfloat16, jnp.float32
    hidden = 4 * width
    return dict(
        low=((layers, 3, tokens, width), low),
        low_small=((layers, 3, tokens, PAD), low),
        heads=((layers, 3, tokens, width), low),
        heads_small=((layers, 3, tokens, PAD), low),
        probs=((layers, H, tokens, tokens), full),
        norm=((layers, 2, tokens, width), full),
        norm_small=((layers, 2, tokens, PAD), full),
        scales=((layers, 4, tokens, LANE), full),
        slope=((layers, tokens, hidden), full),
        slope_small=((layers, tokens, narrow_hidden), full),
        turned=((layers, hidden, tokens), low),
        turned_small=((layers, narrow_hidden, tokens), low),
        small_attn=((layers, 4, PAD, PAD), low),
        small_ff=((layers, 2, narrow_hidden, PAD), low),
    )


SAVED = tuple(saved_shapes(1, 1, 1, 1))


def forward_steps(layer, m, narrow, span):
    tokens, width = m.x.shape
    low = jnp.bfloat16
    vec = lambda row, count=1: m.vectors[pl.ds(layer * VECTOR_ROWS + row, count), :]
    small_vec = lambda row: vec(SMALL_ROW + row)[:, :PAD]

    def embed():
        rows = m.x[...]
        for group in range(LANGS):
            rows = rows + m.onehot[:, group : group + 1] * vec(TABLE_ROW + group)
        m.x[...] = rows
        m.low[layer, 0] = rows.astype(low)
        m.low_small[layer, 0] = m.y[...].astype(low)

    def project_text():
        def body(part, carry):
            joined = dot_nt(m.low[layer, 0], unit_rows(m.attn_w, part))
            bias = jnp.where(part == 0, vec(0), jnp.where(part == 2, vec(1), 0.0))
            m.heads[layer, part] = (joined + bias).astype(low)
            return carry

        lax.fori_loop(0, 3, body, 0)

    def prepare_small():
        permute = natural_rows(span, m.small_raw.shape[3] // m.small_raw_layers).astype(low)
        step = m.small_raw.shape[3] // m.small_raw_layers

        def body(block, carry):
            for member in range(3):
                raw = m.small_raw[
                    block, :, :, pl.ds(layer * step, step), pl.ds(member * PAD, PAD)
                ].reshape(PAD, PAD)
                rows = dot_nn(permute, raw).astype(low)
                if member == 0:
                    m.small_attn[layer, block] = rows
                else:
                    start = pl.multiple_of(block * narrow, 64)
                    m.small_ff[layer, member - 1, pl.ds(start, narrow), :] = rows[:narrow]
            return carry

        lax.fori_loop(0, PLANE, body, 0)

    def project_small():
        for part in range(3):
            joined = dot_nt(m.low_small[layer, 0], m.small_attn[layer, part])
            if part == 0:
                joined = joined + small_vec(0)
            if part == 2:
                joined = joined + small_vec(1)
            m.heads_small[layer, part] = joined.astype(low)
        m.mixed[...] = jnp.zeros_like(m.mixed)

    def attend_pairs(first, count):
        def body(pair, carry):
            lanes = pl.ds(pl.multiple_of(pair * LANE, LANE), LANE)
            query, keyed, valued = (m.heads[layer, n, :, lanes] for n in range(3))
            small_query, small_keyed, small_valued = (m.heads_small[layer, n] for n in range(3))
            lane, small_lane = lane_of((1, LANE)), lane_of((1, PAD))
            same = m.same[...] > 0.0
            contexts = []
            for side in range(2):
                head = 2 * pair + side
                chosen = (lane >= 64 * side) & (lane < 64 * side + 64)
                small_chosen = (small_lane >= 16 * head) & (small_lane < 16 * head + 16)
                mask = jnp.where(chosen, 0.125, 0.0).astype(low)
                small_mask = jnp.where(small_chosen, 0.25, 0.0).astype(low)
                scores = dot_nt(query * mask, keyed) + dot_nt(small_query * small_mask, small_keyed)
                scores = jnp.where(same, scores, MASKED)
                peak = jnp.max(scores, axis=1, keepdims=True)
                powers = jnp.exp(scores - peak)
                probs = powers * (1.0 / jnp.sum(powers, axis=1, keepdims=True))
                m.probs[layer, head] = probs
                probs_low = probs.astype(low)
                contexts.append(dot_nn(probs_low, valued))
                m.mixed[...] += jnp.where(small_chosen, dot_nn(probs_low, small_valued), 0.0)
            m.low[layer, 1, :, lanes] = jnp.where(lane < 64, contexts[0], contexts[1]).astype(low)
            return carry

        lax.fori_loop(first, first + count, body, 0)

    def first_norm():
        m.low_small[layer, 1] = m.mixed[...].astype(low)
        residual = m.x[...] + dot_nt(m.low[layer, 1], unit_rows(m.attn_w, 3)) + vec(2)
        normed, scale = standard(residual, width)
        m.norm[layer, 0] = normed
        m.scales[layer, 0] = jnp.broadcast_to(scale, (tokens, LANE))
        result = normed * vec(4) + vec(5)
        m.normed[...] = result
        m.low[layer, 2] = result.astype(low)

    def first_norm_small():
        branch = dot_nt(m.low_small[layer, 1], m.small_attn[layer, 3]) + small_vec(2)
        normed, scale = standard(m.y[...] + branch, narrow)
        m.norm_small[layer, 0] = normed
        m.scales[layer, 1] = jnp.broadcast_to(scale, (tokens, LANE))
        result = normed * small_vec(4) + small_vec(5)
        m.normed_small[...] = result
        m.low_small[layer, 2] = result.astype(low)

    def activate(column, upper_ref, source, active, slope, turned):
        here = pl.ds(column, LANE)
        value, rate = gelu_parts(upper_ref[:, source])
        slope[layer, :, here] = rate
        value_low = value.astype(low)
        active[:, here] = value_low
        turned[layer, here, :] = value.T.astype(low)

    def up_small():
        m.upper[...] = dot_nt(m.low_small[layer, 2], m.small_ff[layer, 0]) + vec(SMALL_HIDDEN_ROW)

        def body(tile, carry):
            column = pl.multiple_of(tile * LANE, LANE)
            activate(
                column, m.upper, pl.ds(column, LANE), m.active_small, m.slope_small, m.turned_small
            )
            return carry

        lax.fori_loop(0, m.active_small.shape[1] // LANE, body, 0)

    def down_small():
        second = dot_nn(m.active_small[...], m.small_ff[layer, 1]) + small_vec(3)
        normed, scale = standard(m.normed_small[...] + second, narrow)
        m.norm_small[layer, 1] = normed
        m.scales[layer, 3] = jnp.broadcast_to(scale, (tokens, LANE))
        m.y[...] = normed * small_vec(6) + small_vec(7)

    def up_text(first, count):
        def body(block, carry):
            m.upper[...] = dot_nt(m.low[layer, 2], unit_rows(m.up_w, block)) + vec(8 + block)

            def tile_body(tile, inner):
                column = pl.multiple_of(tile * LANE, LANE)
                activate(
                    pl.multiple_of(block * width + column, LANE),
                    m.upper,
                    pl.ds(column, LANE),
                    m.active,
                    m.slope,
                    m.turned,
                )
                return inner

            return lax.fori_loop(0, width // LANE, tile_body, carry)

        lax.fori_loop(first, first + count, body, 0)

    def down_text(first, count):
        def body(block, carry):
            columns = pl.ds(pl.multiple_of(block * width, LANE), width)
            m.second[...] += dot_nn(m.active[:, columns], unit_rows(m.down_w, block))
            return carry

        if first == 0:
            m.second[...] = m.normed[...] + vec(3)
        lax.fori_loop(first, first + count, body, 0)

    def second_norm():
        normed, scale = standard(m.second[...], width)
        m.norm[layer, 1] = normed
        m.scales[layer, 2] = jnp.broadcast_to(scale, (tokens, LANE))
        m.x[...] = normed * vec(6) + vec(7)

    part = H // 4
    after_attn = [(embed, 0.4), (project_text, 1.6)]
    after_small = [(prepare_small, 0.8), (project_small, 0.3)]
    for first in range(0, H // 2, part):
        after_small.append((functools.partial(attend_pairs, first, part), 2.5))
    after_small += [(first_norm, 0.8), (first_norm_small, 0.4), (up_small, 1.0), (down_small, 0.4)]
    after_up = [(functools.partial(up_text, first, 2), 2.4) for first in (0, 2)]
    after_down = [(functools.partial(down_text, first, 2), 0.7) for first in (0, 2)]
    after_down.append((second_norm, 0.3))
    return after_attn, after_small, after_up, after_down


def forward_shapes(layers, depth, tokens, width, narrow, step):
    low, full = jnp.bfloat16, jnp.float32
    span = 4 * width // (PLANE * depth * 2)
    whole = (PLANE, depth, 2, span, width)
    return dict(
        attn_w=(whole, low),
        up_w=(whole, low),
        down_w=(whole, low),
        small_raw=((PLANE, depth, 2, layers * step, width), low),
        own_small=((layers * step, width), low),
        own_small_full=((layers * step, width), full),
        same=((tokens, tokens), full),
        x=((tokens, width), full),
        y=((tokens, PAD), full),
        mixed=((tokens, PAD), full),
        normed=((tokens, width), full),
        normed_small=((tokens, PAD), full),
        upper=((tokens, width), full),
        active=((tokens, 4 * width), low),
        active_small=((tokens, 4 * narrow), low),
        second=((tokens, width), full),
        spread=((3 * SUBLANES, width), full),
    )


FORWARD_SCRATCH = tuple(forward_shapes(1, 1, 1, 1, 1, 1))


def flat_rows(width, narrow):
    rows = [(n, 0, n * width, width) for n in range(PIECE_ROWS)]
    rows += [(TABLE_ROW + n, 1, n * width, width) for n in range(LANGS)]
    rows += [(SMALL_ROW + n, 2, n * narrow, narrow) for n in range(8)]
    return rows + [(SMALL_HIDDEN_ROW, 2, 8 * narrow, 4 * narrow)]


def forward_kernel(depth, layers, narrow, span, *refs):
    refs = list(refs)

    def take(number):
        taken = refs[:number]
        del refs[:number]
        return taken

    count = 3 * layers + 1
    fill = count - 2
    text_attn, text_up, text_down, layout_attn, layout_up, layout_down = take(6)
    pieces = take(3)
    text_in, layout_in, page_row, groups = take(4)
    outs = take(count)
    vector_out, onehot_out, text_out, layout_out = take(4)
    kept = take(len(SAVED))
    own_sem, zs, zr, ps, pr, us, ur, cs, cr, load_sem, keep_sem = take(11)
    all_sum = take(4)
    m = SimpleNamespace()
    for name in SAVED + FORWARD_SCRATCH:
        setattr(m, name, refs.pop(0))
    m.vectors, m.onehot, m.small_raw_layers = vector_out, onehot_out, layers
    at, devices = place(depth)
    dp, z, core, dx, dy, dd = at.dp, at.z, at.core, at.dx, at.dy, at.dd
    half = depth // 2
    low, full = jnp.bfloat16, jnp.float32
    tokens, width = m.x.shape
    step = m.own_small.shape[0] // layers
    vectors = AllSum(devices, vector_out, *all_sum)

    sources = [text_attn.at[0], m.own_small]
    for layer in range(layers):
        if layer > 0:
            sources.append(text_attn.at[layer])
        sources += [text_up.at[layer], text_down.at[layer]]

    def own(k):
        return pltpu.make_async_copy(sources[k], outs[k].at[dp, z, core], own_sem.at[k])

    def line(k, rising, hop, side=0):
        level = z - hop if rising else z + hop
        owner = (dp, dx, dy, dd)[side]
        target = outs[k].at[owner, level, core]
        row = k if side == 0 else count - 1 + side
        return remote(
            sources[k] if hop == 0 and side == 0 else target,
            target,
            zs.at[row, int(rising), hop],
            zr.at[row, level],
            devices.up if rising else devices.down,
        )

    def exists(rising, hop):
        return (z - hop >= 0) if rising else (z + hop < depth)

    def goes_on(rising, hop):
        return exists(rising, hop) & ((z < depth - 1) if rising else (z > 0))

    def unit(rising, hop, to_x):
        level = z - hop if rising else z + hop
        target = outs[0].at[dp, level, core]
        return remote(
            sources[0] if hop == 0 else target,
            target,
            us.at[int(to_x), level],
            ur.at[int(to_x), level],
            devices.x if to_x else devices.y,
        )

    def unit_landed(to_x, level):
        target = outs[0].at[dx if to_x else dy, level, core]
        return remote(
            target, target, us.at[int(to_x), level], ur.at[int(to_x), level], devices.x
        )

    def line_start(k, hop, side=0):
        for rising in (True, False):

            @pl.when(goes_on(rising, hop))
            def start():
                line(k, rising, hop, side).start()

    def line_wait(k, hop, side=0, then=None):
        for rising in (True, False):

            @pl.when(exists(rising, hop))
            def wait():
                line(k, rising, hop, side).wait_recv()
                if then is not None:
                    then(rising, hop)

    def unit_start(rising, hop):
        unit(rising, hop, True).start()
        unit(rising, hop, False).start()

    def plane(k, index, sending=True):
        if k == fill:
            rows = span // 2
            lower, upper = pl.ds(0, rows), pl.ds(rows, rows)
            if sending:
                blocks = ((dp, None), (dp, None), (dx, lower), (dy, upper))
            else:
                blocks = ((dx, None), (dy, None), (dd, lower), (dd, upper))
            owner, rows = blocks[index]
            block = outs[k].at[owner, z, core]
            block = block if rows is None else block.at[rows]
            source = sources[k] if sending and index < 2 else block
        else:
            lower, upper, every = pl.ds(0, half), pl.ds(half, half), pl.ds(0, depth)
            if sending:
                blocks = ((dp, every), (dp, every), (dx, lower), (dy, upper))
            else:
                blocks = ((dx, every), (dy, every), (dd, lower), (dd, upper))
            owner, levels = blocks[index]
            block = outs[k].at[owner, levels, core]
            source = block
        device = (devices.x, devices.y, devices.y, devices.x)[index]
        return remote(source, block, ps.at[k, index], pr.at[k, index], device)

    def across(k, index, side):
        lower, upper, every = pl.ds(0, half), pl.ds(half, half), pl.ds(0, depth)
        if k == fill:
            blocks = ((dp, every), (dx, every), (dy, every), (dd, every))
        else:
            blocks = ((dp, every), (dx, every), (dy, every), (dd, lower), (dd, upper))
        owner, levels = blocks[index]
        block = outs[k].at[owner, levels, side]
        return remote(block, block, cs.at[k, index], cr.at[k, index], devices.core)

    def landed_across(k):
        return range(4 if k == fill else 5)

    held = [m.attn_w, m.small_raw, m.up_w, m.down_w] + [m.attn_w, m.up_w, m.down_w] * (layers - 1)

    def load(k, side):
        owner = (dp, dx, dy, dd)[side]
        return pltpu.make_async_copy(
            outs[k].at[owner], held[k].at[owner], load_sem.at[k, side]
        )

    def loaded(k):
        for side in range(PLANE):
            load(k, side).wait()

    def keep(index, layer):
        source = getattr(m, SAVED[index])
        return pltpu.make_async_copy(
            source.at[layer], kept[index].at[layer], keep_sem.at[index, layer]
        )

    def keep_some(layer, names):
        for name in names:
            keep(SAVED.index(name), layer).start()

    def then_keep(step, layer, names):
        def run():
            step[0]()
            keep_some(layer, names)

        return (run, step[1])

    stages = []
    for layer in range(layers):
        steps = forward_steps(layer, m, narrow, layout_down.shape[1])
        if layer == 0:
            stages += [steps[0], steps[1], steps[2], steps[3]]
        else:
            stages += [steps[0] + steps[1], steps[2], steps[3]]
        stages[-2][-1] = then_keep(stages[-2][-1], layer, SAVED[:5] + SAVED[8:])
        stages[-1][-1] = then_keep(stages[-1][-1], layer, SAVED[5:8])

    def make_small():
        m.own_small_full[...] = jnp.zeros_like(m.own_small_full)
        units = layout_down.shape[1]
        for layer in range(layers):
            rows = pl.ds(layer * step, units)
            m.own_small_full[rows, 0:narrow] = layout_attn[layer].astype(full)
            m.own_small_full[rows, PAD : PAD + narrow] = layout_up[layer].astype(full)
            m.own_small_full[rows, 2 * PAD : 2 * PAD + narrow] = layout_down[layer].astype(full)
        m.own_small[...] = m.own_small_full[...].astype(low)

    def spread_vectors():
        m.spread[...] = jnp.zeros_like(m.spread)
        for n, piece in enumerate(pieces):
            m.spread[pl.ds(SUBLANES * n, layers), 0 : piece.shape[1]] = piece[...].astype(full)
        start = vector_out
        start[...] = jnp.zeros_like(start)
        lane = lane_of((SUBLANES, width))
        for row, n, base, lanes in flat_rows(width, narrow):
            length = pieces[n].shape[1]
            shift = lax.rem(at.me * length - base + 16 * width, width)
            rolled = pltpu.roll(m.spread[pl.ds(SUBLANES * n, SUBLANES), :], shift, 1)
            index = lane + (base - at.me * length)
            inside = (index >= 0) & (index < length) & (lane < lanes)
            rolled = jnp.where(inside, rolled, 0.0)
            for layer in range(layers):
                start[pl.ds(layer * VECTOR_ROWS + row, 1), :] = rolled[layer : layer + 1]
        vectors.send(0)

    def make_masks():
        pages = jnp.broadcast_to(page_row[...].astype(full), (tokens, tokens))
        turned = pages.T
        m.same[...] = jnp.where(pages == turned, 1.0, 0.0)
        group = jnp.where(
            turned == (2 * at.me).astype(full),
            jnp.broadcast_to(groups[:, 0:1], (tokens, tokens)),
            jnp.broadcast_to(groups[:, 1:2], (tokens, tokens)),
        )
        m.onehot[...] = jnp.where(group == lane_of((tokens, tokens)), 1.0, 0.0)

    def take_in():
        m.x[...] = text_in[...].astype(full)
        m.y[...] = jnp.zeros_like(m.y)
        m.y[:, 0:narrow] = layout_in[...].astype(full).T

    def land(k, sides):
        for side in sides:
            across(k, side, 1 - core).wait_recv()
            if side == 3 and k != fill:
                across(k, 4, 1 - core).wait_recv()
            load(k, side).start()

    signal(devices)
    make_small()
    greeted()
    for k in (0, fill, 1):
        own(k).start()
    line_start(0, 0)
    unit_start(True, 0)
    plane(fill, 0).start()
    plane(fill, 1).start()
    for k in range(2, count):
        if k != fill:
            own(k).start()

    plan = Plan()
    chain = [k for k in range(count) if k != fill]
    size = [sources[k].shape[0] / UNIT_ROWS_PER_US for k in range(count)]

    def begin_line(k, side):
        if side == 0:
            own(k).wait()
        if k > 0:
            line_start(k, 0, side)

    def next_line(k, hop, side):
        line_wait(k, hop, side, unit_start if k == 0 else None)
        if hop < depth - 1:
            line_start(k, hop, side)

    def add_line(k, side, after, needs, rank):
        sends = [("z", size[k], ("z", 1, k, side))]
        if k == 0:
            sends += [("x", size[k], ("u", 0)), ("x", size[fill], ("f", 1))]
        plan.add(("z", 0, k, side), functools.partial(begin_line, k, side), after, needs, sends, 0.3, rank)
        for hop in range(1, depth):
            sends = []
            if hop < depth - 1:
                sends.append(("z", size[k], ("z", hop + 1, k, side)))
            if k == 0:
                sends.append(("x", size[k], ("u", hop)))
            plan.add(
                ("z", hop, k, side),
                functools.partial(next_line, k, hop, side),
                [("z", hop - 1, k, side)],
                [("z", hop, k, side)],
                sends,
                0.3,
                rank,
            )

    def plane_first(k):
        if k > 0:
            plane(k, 0).start()
            plane(k, 1).start()
        across(k, 0, core).start()

    def plane_second(k):
        for index in (0, 1):
            if k == 0:
                for level in range(depth):
                    unit_landed(index == 0, level).wait_recv()
            else:
                plane(k, index, False).wait_recv()
            plane(k, index + 2).start()
            if k != fill:
                across(k, index + 1, core).start()

    def plane_third(k):
        for index in (2, 3):
            plane(k, index, False).wait_recv()
            if k != fill:
                across(k, index + 1, core).start()

    def cross_fill(side):
        across(fill, side, core).start()

    last = {}
    lines = [(k, 0) for k in chain]
    for side in range(4):
        lines.insert((4, 6, 7, 9)[side], (fill, side))
    for n, (k, side) in enumerate(lines):
        after = [("z", 1 if n > 1 else 2) + lines[n - 1]] if n else []
        if k == fill:
            after.append(("p", 2 if side < 3 else 3, fill))
        add_line(k, side, after, [], 10 * n)
    for n, k in enumerate(chain):
        arrive = ("x", k) if k else ("u", depth - 1)
        sends = [("c", 0.4 * size[k], ("c", 0, k))]
        if k:
            sends.append(("x", 4 * size[k], arrive))
        plan.add(("p", 1, k), functools.partial(plane_first, k), [("z", depth - 1, k, 0)], [], sends, 0.2, 10 * n + 1)
        sends = [("x", 2 * size[k], ("d", k)), ("c", 0.8 * size[k], ("c", 1, k))]
        plan.add(("p", 2, k), functools.partial(plane_second, k), [("p", 1, k)], [arrive], sends, 0.2, 10 * n + 2)
        sends = [("c", 0.4 * size[k], ("c", 2, k))]
        plan.add(("p", 3, k), functools.partial(plane_third, k), [("p", 2, k)], [("d", k)], sends, 0.2, 10 * n + 3)
    plan.add(
        ("p", 2, fill),
        functools.partial(plane_second, fill),
        [("z", 1, 0, 0)],
        [("f", 1)],
        [("x", size[fill] / 2, ("f", 2))],
        0.2,
        5,
    )
    plan.add(("p", 3, fill), functools.partial(plane_third, fill), [("p", 2, fill)], [("f", 2)], rank=6)
    for side in range(4):
        plan.add(
            ("a", side),
            functools.partial(cross_fill, side),
            [("z", depth - 1, fill, side)],
            [],
            [("c", 0.4 * size[fill], ("a", side))],
            0.1,
            25 + 10 * side,
        )
    previous = None
    vector_steps = [spread_vectors]
    vector_steps += [functools.partial(vectors.advance, n) for n in range(AllSum.STEPS)]
    for n, step_of in enumerate(vector_steps):
        link, amount = (("c", 0.3), ("z", 2.2), ("z", 6.0), ("x", 2.2), ("x", 2.2), ("h", 0.0))[n]
        sends = [(link, amount, ("v", n))]
        needs = [("v", n - 1)] if n else []
        after = [("v", n - 1)] if n else []
        if n == 1:
            after.append(("z", 2, 0, 0))
        plan.add(("v", n), step_of, after, needs, sends, 0.1 if n else 0.5, 2)
    plan.add("i", take_in, [("v", 0)], time=0.1, rank=3)
    plan.add("m", make_masks, ["i"], time=0.1, rank=3)
    previous = [("v", AllSum.STEPS), "m"]
    for k in range(count):
        vacant = [last[k - 3]] if k > 3 else []
        if k == fill:
            landed = [("a", side) for side in range(4)]
            plan.add(("l", k), functools.partial(land, k, range(4)), landed + vacant, landed, [("h", 2.4, ("h", k))], 0.2, 10 * k)
        else:
            landed = [("c", 0, k), ("c", 1, k)]
            plan.add(("k", k), functools.partial(land, k, range(3)), [("p", 2, k)] + vacant, landed, [("h", 2.0, ("k", k))], 0.2, 10 * k)
            plan.add(("l", k), functools.partial(land, k, (3,)), [("p", 3, k), ("k", k)], [("c", 2, k)], [("h", 0.7, ("h", k))], 0.2, 10 * k)
        for n, (closure, time) in enumerate(stages[k]):
            run = closure
            if n == 0:
                run = functools.partial(lambda k, closure: (loaded(k), closure()), k, closure)
            plan.add(("s", k, n), run, previous + [("l", k)], [("h", k)], (), time, 1000 + k, True)
            previous = [("s", k, n)]
        last[k] = previous[0]
    plan.run()
    text_out[...] = m.x[...]
    layout_out[...] = m.y[:, 0:narrow].T
    vectors.close()
    for index in range(len(SAVED)):
        for layer in range(layers):
            keep(index, layer).wait()
    for level in range(depth):
        for to_x in (True, False):
            unit_landed(to_x, level).wait_send()
    for k in range(count):
        for index in landed_across(k):
            across(k, index, core).wait_send()
        for index in range(4):
            if k > 0 or index > 1:
                plane(k, index).wait_send()
        for rising in (True, False):
            for hop in range(depth):

                @pl.when(goes_on(rising, hop))
                def drain():
                    for side in range(4 if k == fill else 1):
                        line(k, rising, hop, side).wait_send()


def run_forward(depth, narrow, step, weights, pieces, text_in, layout_in, page_row, groups):
    dma = pltpu.SemaphoreType.DMA
    tokens, width = text_in.shape
    layers, span, unused = weights[0].shape
    count = 3 * layers + 1
    full = jnp.float32
    saved = saved_shapes(layers, tokens, width, 4 * narrow)
    scratch = forward_shapes(layers, depth, tokens, width, narrow, step)
    rows = [span, layers * step] + [span] * (count - 2)
    vector_shape = (layers * VECTOR_ROWS, width)
    results = pl.pallas_call(
        functools.partial(forward_kernel, depth, layers, narrow, span),
        out_shape=[
            jax.ShapeDtypeStruct((PLANE, depth, 2, row, width), weights[0].dtype) for row in rows
        ]
        + [
            jax.ShapeDtypeStruct(vector_shape, full),
            jax.ShapeDtypeStruct((tokens, LANE), full),
            jax.ShapeDtypeStruct((tokens, width), full),
            jax.ShapeDtypeStruct((narrow, tokens), full),
        ]
        + [jax.ShapeDtypeStruct(*saved[name]) for name in SAVED],
        in_specs=[IN_VMEM] * 13,
        out_specs=[ANY] * count + [IN_VMEM] * 4 + [ANY] * len(SAVED),
        scratch_shapes=[
            dma((count,)),
            dma((count + 3, 2, depth)),
            dma((count + 3, depth)),
            dma((count, 4)),
            dma((count, 4)),
            dma((2, depth)),
            dma((2, depth)),
            dma((count, 5)),
            dma((count, 5)),
            dma((count, PLANE)),
            dma((len(SAVED), layers)),
        ]
        + AllSum.scratch(vector_shape)
        + [pltpu.VMEM(*saved[name]) for name in SAVED]
        + [pltpu.VMEM(*scratch[name]) for name in FORWARD_SCRATCH],
        compiler_params=pltpu.CompilerParams(
            collective_id=0, has_side_effects=True, vmem_limit_bytes=66000000
        ),
        name="forward_blocks",
    )(*weights, *pieces, text_in, layout_in, page_row, groups)
    return results[:count], results[count : count + 4], results[count + 4 :]


TEXT_MEMBERS = 3
LINKS = 10


def back_shapes(layers, depth, tokens, width, narrow_hidden):
    low, full = jnp.bfloat16, jnp.float32
    span = 4 * width // (PLANE * depth * 2)
    unit = (PLANE, depth, span, LANE)
    whole = (PLANE, depth, 2, span, LANE)
    return dict(
        weights=((2, PLANE, depth, 2, span, width), low),
        gx=((tokens, width), full),
        gy=((tokens, PAD), full),
        down_low=((tokens, width), low),
        down_low_small=((tokens, PAD), low),
        branch_low=((tokens, width), low),
        branch_low_small=((tokens, PAD), low),
        wide=((tokens, width), full),
        upper_low=((tokens, 4 * width), low),
        upper_low_small=((tokens, narrow_hidden), low),
        context=((tokens, width), low),
        context_small=((tokens, PAD), low),
        joined=((3, tokens, width), low),
        mixed=((3, tokens, PAD), full),
        rows_up=(whole, low),
        rows_attn=(whole, low),
        rows_small=((2, narrow_hidden, tokens), low),
        in_land=((layers, 4, tokens, width), low),
        in_land_small=((layers, 4, tokens, PAD), low),
        rows_land=((layers, 3) + unit, low),
        rows_land_small=((layers, 3, narrow_hidden, tokens), low),
        sums=((layers * VECTOR_ROWS, width), full),
    )


BACK_SCRATCH = tuple(back_shapes(1, 1, 1, 1, 1))


def standard_back(grad, normed, scale, gain, width):
    pushed = grad * gain
    average = jnp.sum(pushed, axis=1, keepdims=True) * (1.0 / width)
    along = jnp.sum(pushed * normed, axis=1, keepdims=True) * (1.0 / width)
    result = scale * (pushed - average - normed * along)
    if grad.shape[1] != width:
        result = jnp.where(lane_of(grad.shape) < width, result, 0.0)
    return result, total(grad * normed), total(grad)


def total(rows):
    return jnp.sum(rows.astype(jnp.float32), axis=0, keepdims=True)


def padded_rows_of_core(span, step, core):
    units = PAD // step // 2
    shape = (units * step, units * 2 * span)
    row = lax.broadcasted_iota(jnp.int32, shape, 0)
    column = lax.broadcasted_iota(jnp.int32, shape, 1)
    unit = jnp.zeros(shape, jnp.int32)
    for n in range(1, units):
        unit = unit + jnp.where(row >= n * step, 1, 0)
    inside = row - unit * step
    source = (2 * unit + core) * span + inside
    return jnp.where((source == column) & (inside < span), 1.0, 0.0)


def backward_kernel(depth, layers, narrow, span, step, *refs):
    refs = list(refs)

    def take(number):
        taken = refs[:number]
        del refs[:number]
        return taken

    text_count = TEXT_MEMBERS * layers
    count = (TEXT_MEMBERS + 1) * layers
    gathered = take(text_count)
    kept = take(len(SAVED))
    vec_ref, text_cot, layout_cot, onehot = take(4)
    finals = take(count)
    vector_out, text_out, layout_out = take(3)
    m = SimpleNamespace()
    for name in SAVED + BACK_SCRATCH:
        setattr(m, name, refs.pop(0))
    mine_text, mine_small = take(2)
    landed_diag, landed_plane, landed_line = take(count), take(count), take(count)
    outs = take(count)
    weight_sem, keep_sem, out_sem, xs, xr, ps, pr, zs, zr = take(9)
    all_sum = take(4)
    at, devices = place(depth)
    dp, z, core, dx, dy, dd = at.dp, at.z, at.core, at.dx, at.dy, at.dd
    fill = 1
    owners = (dp, dx, dy, dd)
    half = depth // 2
    low = jnp.bfloat16
    tokens, width = m.gx.shape
    hidden_small = m.upper_low_small.shape[1]
    signal(devices)
    greeted()
    vectors = AllSum(devices, vector_out, *all_sum)

    slots, reuse = {}, {}
    for k in range(count):
        if k % 4 != 3:
            spare = [n for n in range(mine_text.shape[0]) if n not in slots.values()]
            if spare:
                slots[k] = spare[0]
            else:
                reuse[k] = min(n for n in slots if n != fill and n not in reuse.values())
                slots[k] = slots[reuse[k]]

    def mine(k):
        if k % 4 == 3:
            return mine_small.at[k // 4]
        return mine_text.at[slots[k]]

    order = []
    for layer in reversed(range(layers)):
        order += [3 * layer + 2, 3 * layer + 1, 3 * layer]

    def weight_load(index):
        return pltpu.make_async_copy(
            gathered[order[index]], m.weights.at[index % 2], weight_sem.at[index]
        )

    def saved_load(name, layer):
        index = SAVED.index(name)
        return pltpu.make_async_copy(
            kept[index].at[layer], getattr(m, name), keep_sem.at[index, layer]
        )

    def cross(layer, link):
        moves = (
            (m.low, m.in_land.at[layer, pl.ds(0, 3)]),
            (m.turned.at[:, :, 1 - core], m.rows_land.at[layer, 0]),
            (m.down_low, m.in_land.at[layer, 3]),
            (m.rows_up.at[:, :, 1 - core], m.rows_land.at[layer, 1]),
            (m.rows_attn.at[:, :, 1 - core], m.rows_land.at[layer, 2]),
            (m.low_small, m.in_land_small.at[layer, pl.ds(0, 3)]),
            (m.turned_small, m.rows_land_small.at[layer, 0]),
            (m.down_low_small, m.in_land_small.at[layer, 3]),
            (m.rows_small.at[0], m.rows_land_small.at[layer, 1]),
            (m.rows_small.at[1], m.rows_land_small.at[layer, 2]),
        )
        source, target = moves[link]
        return remote(
            source, target, xs.at[layer, link], xr.at[layer, link], devices.core
        )

    def plane(k, index):
        if k == fill:
            size = landed_diag[k].shape[1]
            lower, upper = pl.ds(0, size), pl.ds(size, size)
            own = lambda owner, rows: mine(k).at[owner, z, rows]
        else:
            lower, upper = pl.ds(0, half), pl.ds(half, half)
            own = lambda owner, levels: mine(k).at[owner, levels]
        diag, direct = landed_diag[k], landed_plane[k]
        moves = (
            (dd, lower, diag.at[0], devices.y),
            (dd, upper, diag.at[1], devices.x),
            (dx, upper, direct.at[0, upper], devices.x),
            (dy, lower, direct.at[1, lower], devices.y),
            (dx, lower, direct.at[0, lower], devices.x),
            (dy, upper, direct.at[1, upper], devices.y),
        )
        owner, part, target, device = moves[index]
        return remote(own(owner, part), target, ps.at[k, index], pr.at[k, index], device)

    def line(k, rising, level, slot, side=0):
        row = k if side == 0 else count - 1 + side
        return remote(
            mine(k).at[owners[side], level],
            landed_line[k].at[slot, side],
            zs.at[row, int(rising), level],
            zr.at[row, int(rising), level],
            devices.up if rising else devices.down,
        )

    def second_sums(k):
        if k == fill:
            size = landed_diag[k].shape[1]
            lower, upper = pl.ds(0, size), pl.ds(size, size)
            one, other = mine(k).at[dx, z, lower], mine(k).at[dy, z, upper]
            add = add_rows
        else:
            one = mine(k).at[dx, pl.ds(0, half)]
            other = mine(k).at[dy, pl.ds(half, half)]
            add = add_units
        plane(k, 0).wait_recv()
        add(one, landed_diag[k].at[0])
        plane(k, 4).start()
        plane(k, 1).wait_recv()
        add(other, landed_diag[k].at[1])
        plane(k, 5).start()

    def third_sums(k):
        for index in (2, 3, 4, 5):
            plane(k, index).wait_recv()
        if k == fill:
            result = mine(k)[dp, z].astype(jnp.float32)
            for side in range(2):
                result = result + landed_plane[k][side].astype(jnp.float32)
            outs[k][...] = result
            put_out(k).start()
        else:
            add_units(mine(k).at[dp], landed_plane[k].at[0], landed_plane[k].at[1])
            line_step(k, 0)

    def passed(rising, hop):
        return range(hop + 1, depth) if rising else range(depth - 1 - hop)

    def line_step(k, hop, side=0):
        for rising in (True, False):

            @pl.when(z == (hop if rising else depth - 1 - hop))
            def move():
                for level in passed(rising, hop):
                    if hop > 0:
                        line(k, rising, level, level, side).wait_recv()
                        add_rows(mine(k).at[owners[side], level], landed_line[k].at[level, side])
                    last = rising and level == hop + 1
                    line(k, rising, level, depth if last else level, side).start()

    def last_sums(k, side=0):
        if k != fill:
            outs[k][...] = mine(k)[dp, z].astype(jnp.float32)
        for rising in (True, False):

            @pl.when((z > 0) if rising else (z < depth - 1))
            def add():
                slot = depth if rising else z
                line(k, rising, z, slot, side).wait_recv()
                if k == fill:
                    add_rows(mine(k).at[owners[side], z], landed_line[k].at[slot, side])
                else:
                    outs[k][...] += landed_line[k][slot, side].astype(jnp.float32)

        if k != fill:
            put_out(k).start()

    def put_out(k):
        return pltpu.make_async_copy(outs[k], finals[k], out_sem.at[k])

    def fill_plane():
        for index in range(4):
            plane(fill, index).start()

    def drain(k):
        for index in range(6):
            plane(k, index).wait_send()
        for hop in range(depth - 1):
            for rising in (True, False):

                @pl.when(z == (hop if rising else depth - 1 - hop))
                def wait():
                    for level in passed(rising, hop):
                        for side in range(PLANE if k == fill else 1):
                            line(k, rising, level, level, side).wait_send()

    plan = Plan()
    size = [outs[k].shape[0] / UNIT_ROWS_PER_US for k in range(count)]

    def add_scatter(k, rank):
        one = size[k]

        def step(hop, side):
            if hop < depth - 1:
                line_step(k, hop, side)
            else:
                last_sums(k, side)

        for side in range(PLANE if k == fill else 1):
            for hop in range(0 if k == fill else 1, depth):
                sends = []
                if hop < depth - 1:
                    sends.append((("z", hop), (depth - 1 - hop) * one, ("z", hop + 1, k, side)))
                after = [("z", hop - 1, k, side)] if hop else [("o", k)]
                if k != fill and hop == 1:
                    after = [("s", 3, k)]
                if k == fill and hop == 0 and side:
                    after.append(("z", 1, k, side - 1))
                needs = [("z", hop, k, side)] if hop else []
                plan.add(
                    ("z", hop, k, side), functools.partial(step, hop, side), after, needs, sends, 0.3, rank
                )
        first = ("o", k)
        share = 2 * one
        if k == fill:
            first, share = ("f", 0), one / 2
            sends = [("x", share, ("d", k)), ("x", share, ("e", k))]
            ends = [("z", depth - 1, k, side) for side in range(PLANE)]
            plan.add(first, fill_plane, ends, [], sends, 0.2, rank)
        plan.add(
            ("s", 2, k), functools.partial(second_sums, k), [first], [("d", k)], [("x", share, ("g", k))], 0.5, rank
        )
        sends = [(("z", 0), (depth - 1) * one, ("z", 1, k, 0))] if k != fill else []
        plan.add(
            ("s", 3, k), functools.partial(third_sums, k), [("s", 2, k)], [("e", k), ("g", k)], sends, 1.0, rank
        )

    def own_sends(k):
        if k == fill:
            return []
        return [("x", 2 * size[k], ("d", k)), ("x", 2 * size[k], ("e", k))]

    previous = []

    def then(name, run, time, needs=(), sends=(), after=()):
        plan.add(name, run, previous + list(after), needs, sends, time, 1000, True)
        previous[:] = [name]

    def done(k):
        return [("s", 3, k), ("z", depth - 1, k, 0)]

    def own_sums(k, rows, rows_land, ins, ins_land):
        if k in reuse:
            drain(reuse[k])

        def block(turn, carry):
            owner = jnp.where(turn == 0, dd, jnp.where(turn == 1, dx, jnp.where(turn == 2, dy, dp)))
            left = jnp.concatenate(
                [
                    rows[owner, :, core].reshape(-1, tokens),
                    rows_land[owner].reshape(-1, tokens),
                ],
                axis=1,
            )
            right = jnp.concatenate([ins(owner), ins_land(owner)], axis=0)
            result = dot_nn(left, right)
            mine(k)[owner] = result.astype(low).reshape(depth, -1, width)
            if k != fill:
                for index, when in enumerate((0, 0, 1, 2)):

                    @pl.when(turn == when)
                    def send():
                        plane(k, index).start()

            return carry

        lax.fori_loop(0, PLANE, block, 0)

    m.gx[...] = text_cot[...].astype(jnp.float32)
    m.gy[...] = jnp.zeros_like(m.gy)
    m.gy[:, 0:narrow] = layout_cot[...].astype(jnp.float32).T
    first_names = ("norm", "scales", "turned", "norm_small", "turned_small", "slope", "low")
    names = first_names + tuple(name for name in SAVED if name not in first_names)
    weight_load(0).start()
    for name in names:
        saved_load(name, layers - 1).start()
    weight_load(1).start()

    def add_layer(turn, layer):
        k = 4 * turn
        vec = lambda row, n=1: vec_ref[pl.ds(layer * VECTOR_ROWS + row, n), :]
        small_vec = lambda row: vec(SMALL_ROW + row)[:, :PAD]
        slot = lambda member: m.weights.at[(3 * turn + member) % 2]

        def put(row, value):
            m.sums[pl.ds(layer * VECTOR_ROWS + row, 1), :] = value

        def put_small(row, value):
            m.sums[pl.ds(layer * VECTOR_ROWS + SMALL_ROW + row, 1), :PAD] = value


        def tail():
            m.sums[pl.ds(layer * VECTOR_ROWS + SMALL_ROW, VECTOR_ROWS - SMALL_ROW), :] = jnp.zeros(
                (VECTOR_ROWS - SMALL_ROW, width), jnp.float32
            )
            for name in ("norm", "scales", "turned"):
                saved_load(name, layer).wait()
            cross(layer, 1).start()
            grad, gain_sum, shift_sum = standard_back(
                m.gx[...], m.norm[1], m.scales[2][:, :1], vec(6), width
            )
            put(6, gain_sum)
            put(7, shift_sum)
            m.gx[...] = grad
            m.down_low[...] = grad.astype(low)
            cross(layer, 2).start()
            put(3, total(m.down_low[...]))

        def tail_small():
            for name in ("norm_small", "turned_small"):
                saved_load(name, layer).wait()
            cross(layer, 6).start()
            grad, gain_sum, shift_sum = standard_back(
                m.gy[...], m.norm_small[1], m.scales[3][:, :1], small_vec(6), narrow
            )
            put_small(6, gain_sum)
            put_small(7, shift_sum)
            m.gy[...] = grad
            m.down_low_small[...] = grad.astype(low)
            cross(layer, 7).start()
            put_small(3, total(m.down_low_small[...]))

        def own_down():
            cross(layer, 1).wait_recv()
            cross(layer, 2).wait_recv()
            own_sums(
                k,
                m.turned,
                m.rows_land.at[layer, 0],
                lambda owner: m.down_low[...],
                lambda owner: m.in_land[layer, 3],
            )

        cut = 3 * LANE

        def hidden(block, carry):
            m.wide[...] = dot_nt(m.down_low[...], unit_rows(slot(0), block))
            for side in range(width // cut):
                inside = pl.ds(side * cut, cut)
                columns = pl.ds(pl.multiple_of(block * width + side * cut, LANE), cut)
                rows = m.slope[:, columns] * m.wide[:, inside]
                rows_low = rows.astype(low)
                m.upper_low[:, columns] = rows_low
                m.sums[pl.ds(layer * VECTOR_ROWS + 8 + block, 1), inside] = total(rows_low)
                levels = depth * cut // width
                m.rows_up[block, pl.ds(side * levels, levels)] = (
                    rows.T.astype(low).reshape(levels, 2, -1, tokens)
                )
            return carry


        def hidden_blocks(first, number):
            if first == 0:
                for name in names[5:]:
                    saved_load(name, layer).wait()
                cross(layer, 0).start()
                cross(layer, 5).start()
                weight_load(3 * turn).wait()
            lax.fori_loop(first, first + number, hidden, 0)
            if first + number == PLANE:
                cross(layer, 3).start()
                if 3 * turn + 2 < 3 * layers:
                    weight_load(3 * turn + 2).start()

        def hide_small():
            m.wide[...] = dot_nt(m.down_low_small[...], m.small_ff[1])

            for side in range(hidden_small // cut):
                columns = pl.ds(side * cut, cut)
                rows = m.slope_small[:, columns] * m.wide[:, columns]
                rows_low = rows.astype(low)
                m.upper_low_small[:, columns] = rows_low
                m.rows_small[0, columns, :] = rows.T.astype(low)
                m.sums[
                    pl.ds(layer * VECTOR_ROWS + SMALL_HIDDEN_ROW, 1), columns
                ] = total(rows_low)
            cross(layer, 8).start()

        def own_up():
            cross(layer, 0).wait_recv()
            cross(layer, 3).wait_recv()
            own_sums(
                k + 1,
                m.rows_up,
                m.rows_land.at[layer, 1],
                lambda owner: m.low[2],
                lambda owner: m.in_land[layer, 2],
            )

        def lower_text():
            weight_load(3 * turn + 1).wait()

            def lower(block, carry):
                columns = pl.ds(pl.multiple_of(block * width, LANE), width)
                m.gx[...] += dot_nn(m.upper_low[:, columns], unit_rows(slot(1), block))
                return carry

            lax.fori_loop(0, PLANE, lower, 0)
            if 3 * turn + 3 < 3 * layers:
                weight_load(3 * turn + 3).start()
            grad, gain_sum, shift_sum = standard_back(
                m.gx[...], m.norm[0], m.scales[0][:, :1], vec(4), width
            )
            put(4, gain_sum)
            put(5, shift_sum)
            m.gx[...] = grad
            m.branch_low[...] = grad.astype(low)
            put(2, total(m.branch_low[...]))
            for side in range(width // cut):
                levels = depth * cut // width
                tile = m.gx[:, side * cut : (side + 1) * cut]
                m.rows_attn[3, pl.ds(side * levels, levels)] = (
                    tile.T.astype(low).reshape(levels, 2, -1, tokens)
                )

        def lower_small():
            grad = m.gy[...] + dot_nn(m.upper_low_small[...], m.small_ff[0])
            grad, gain_sum, shift_sum = standard_back(
                grad, m.norm_small[0], m.scales[1][:, :1], small_vec(4), narrow
            )
            put_small(4, gain_sum)
            put_small(5, shift_sum)
            m.gy[...] = grad
            m.branch_low_small[...] = grad.astype(low)
            put_small(2, total(m.branch_low_small[...]))
            m.rows_small[1, pl.ds(3 * narrow, narrow), :] = grad.T[:narrow].astype(low)

        def contexts():
            weight_load(3 * turn + 2).wait()
            m.context[...] = dot_nn(m.branch_low[...], unit_rows(slot(2), 3)).astype(low)
            m.context_small[...] = dot_nn(m.branch_low_small[...], m.small_attn[3]).astype(low)
            m.mixed[...] = jnp.zeros_like(m.mixed)

        def pair_back(pair, carry):
            lanes = pl.ds(pl.multiple_of(pair * LANE, LANE), LANE)
            query, keyed, valued = (m.heads[n, :, lanes] for n in range(3))
            small_query, small_keyed, small_valued = (m.heads_small[n] for n in range(3))
            context, context_small = m.context[:, lanes], m.context_small[...]
            lane, small_lane = lane_of((1, LANE)), lane_of((1, PAD))
            results = []
            for side in range(2):
                head = 2 * pair + side
                chosen = (lane >= 64 * side) & (lane < 64 * side + 64)
                small_chosen = (small_lane >= 16 * head) & (small_lane < 16 * head + 16)
                mask = jnp.where(chosen, 1.0, 0.0).astype(low)
                small_mask = jnp.where(small_chosen, 1.0, 0.0).astype(low)
                probs = m.probs[head]
                grad_probs = dot_nt(context * mask, valued) + dot_nt(
                    context_small * small_mask, small_valued
                )
                inner = jnp.sum(grad_probs * probs, axis=1, keepdims=True)
                scores = probs * (grad_probs - inner)
                scores_low = scores.astype(low)
                scores_turned = scores.T.astype(low)
                probs_turned = probs.T.astype(low)
                results.append(
                    (
                        dot_nn(scores_low, keyed) * 0.125,
                        dot_nn(scores_turned, query) * 0.125,
                        dot_nn(probs_turned, context),
                    )
                )
                small = (
                    dot_nn(scores_low, small_keyed) * 0.25,
                    dot_nn(scores_turned, small_query) * 0.25,
                    dot_nn(probs_turned, context_small),
                )
                for n in range(3):
                    m.mixed[n] += jnp.where(small_chosen, small[n], 0.0)
            for n in range(3):
                m.joined[n, :, lanes] = jnp.where(lane < 64, results[0][n], results[1][n]).astype(
                    low
                )
            return carry


        def pairs(first, number):
            lax.fori_loop(first, first + number, pair_back, 0)

        def turn_rows():
            for part in range(3):
                for side in range(width // cut):
                    levels = depth * cut // width
                    tile = m.joined[part, :, side * cut : (side + 1) * cut].astype(jnp.float32)
                    m.rows_attn[part, pl.ds(side * levels, levels)] = (
                        tile.T.astype(low).reshape(levels, 2, -1, tokens)
                    )
                tile = m.mixed[part].astype(low).astype(jnp.float32)
                m.rows_small[1, pl.ds(part * narrow, narrow), :] = tile.T[:narrow].astype(low)
            cross(layer, 4).start()
            cross(layer, 9).start()
            put(0, total(m.joined[0]))
            put(1, total(m.joined[2]))
            put_small(0, total(m.mixed[0].astype(low)))
            put_small(1, total(m.mixed[2].astype(low)))

        def entering(part, carry):
            m.gx[...] += dot_nn(m.joined[part], unit_rows(slot(2), part))
            return carry


        def attn_sums():
            cross(layer, 4).wait_recv()
            own_sums(
                k + 2,
                m.rows_attn,
                m.rows_land.at[layer, 2],
                lambda owner: m.low[jnp.where(owner == PLANE - 1, 1, 0)],
                lambda owner: m.in_land[layer, jnp.where(owner == PLANE - 1, 1, 0)],
            )


        def enter():
            lax.fori_loop(0, 3, entering, 0)
            if 3 * turn + 4 < 3 * layers:
                weight_load(3 * turn + 4).start()
            grad = m.gy[...]
            for part in range(3):
                grad = grad + dot_nn(m.mixed[part].astype(low), m.small_attn[part])
            m.gy[...] = grad
            for group in range(LANGS):
                put(TABLE_ROW + group, total(onehot[:, group : group + 1] * m.gx[...]))
            if layer == 0:
                text_out[...] = m.gx[...]
                layout_out[...] = m.gy[:, 0:narrow].T
                vector_out[...] = m.sums[...]
                vectors.send(0)

        def small_sums():
            for link in (5, 6, 7, 8, 9):
                cross(layer, link).wait_recv()
            arrange = padded_rows_of_core(span, step, core).astype(low)
            small_rows = (m.rows_small.at[1], m.rows_small.at[0], m.turned_small)
            small_land = (2, 1, 0)
            for member in range(3):
                for block in range(PLANE):
                    rows = pl.ds(block * narrow, narrow)
                    source = (1 if block == PLANE - 1 else 0, 2, 3)[member]
                    own_in = m.down_low_small[...] if member == 2 else m.low_small[source]
                    left = jnp.concatenate(
                        [
                            small_rows[member][rows, :],
                            m.rows_land_small[layer, small_land[member], rows, :],
                        ],
                        axis=1,
                    )
                    right = jnp.concatenate([own_in, m.in_land_small[layer, source]], axis=0)
                    placed = dot_nn(arrange, dot_nn(left, right).astype(low)).astype(low)
                    mine(k + 3)[block, :, :, pl.ds(member * PAD, PAD)] = placed.reshape(
                        depth, step, PAD
                    )
            if layer > 0:
                for link in range(LINKS):
                    cross(layer, link).wait_send()
                for name in names:
                    saved_load(name, layer - 1).start()
            for index in range(4):
                plane(k + 3, index).start()

        own = lambda n: ("o", k + n)
        crossed = lambda link: ("c", layer, link)
        free = lambda n: done(reuse[k + n]) if k + n in reuse else []
        then(("t", 0, turn), tail, 1.7, sends=[("c", 1.0, crossed(1)), ("c", 0.5, crossed(2))])
        then(("t", 1, turn), tail_small, 0.2, sends=[("c", 0.8, crossed(6))])
        then(own(0), own_down, 1.4, [crossed(1), crossed(2)], own_sends(k), free(0))
        add_scatter(k, 4 * k)
        then(
            ("h", 0, turn), functools.partial(hidden_blocks, 0, 2), 1.4, sends=[("c", 1.5, crossed(0))]
        )
        then(
            ("h", 1, turn), functools.partial(hidden_blocks, 2, 2), 1.3, sends=[("c", 1.0, crossed(3))]
        )
        then(("h", 2, turn), hide_small, 0.4, sends=[("c", 0.5, crossed(8))])
        then(own(1), own_up, 1.4, [crossed(0), crossed(3)], own_sends(k + 1), free(1))
        add_scatter(k + 1, 4 * k + 4)
        then(("n", 0, turn), lower_text, 1.7)
        then(("n", 1, turn), lower_small, 0.4)
        then(("n", 2, turn), contexts, 0.4)
        then(("p", 0, turn), functools.partial(pairs, 0, H // 4), 2.7)
        then(("p", 1, turn), functools.partial(pairs, H // 4, H // 4), 2.7)
        then(("r", turn), turn_rows, 0.4, sends=[("c", 1.0, crossed(4)), ("c", 0.5, crossed(9))])
        then(own(2), attn_sums, 1.4, [crossed(4)], own_sends(k + 2), free(2))
        add_scatter(k + 2, 4 * k + 8)
        then(("e", turn), enter, 1.4, sends=[("c", 0.3, ("v", 0))] if layer == 0 else [])
        late = [("s", 2, k + 2)] if layer == 0 else []
        then(own(3), small_sums, 2.6, [crossed(9)], own_sends(k + 3), late)
        add_scatter(k + 3, 4 * k + 12)

    for turn, layer in enumerate(reversed(range(layers))):
        add_layer(turn, layer)
    for n in range(AllSum.STEPS):
        sends = [((("z", 0), 2.2), (("z", 0), 4.4), ("x", 2.2), ("x", 2.2), ("c", 0.0))[n] + (("v", n + 1),)]
        after = [("v", n - 1)] if n else [("e", layers - 1)]
        plan.add(("v", n), functools.partial(vectors.advance, n), after, [("v", n)], sends, 0.2, -1)
    plan.run()
    vectors.close()
    for link in range(LINKS):
        cross(0, link).wait_send()
    drained = list(reuse.values())
    for k in range(count):
        put_out(k).wait()
    for k in range(count):
        if k not in drained:
            drain(k)


def run_backward(depth, layers, narrow, span, step, gathered, saved, vectors, text_cot, layout_cot, onehot):
    dma = pltpu.SemaphoreType.DMA
    tokens, width = text_cot.shape
    low, full = jnp.bfloat16, jnp.float32
    shapes = back_shapes(layers, depth, tokens, width, 4 * narrow)
    unit = gathered[0].shape[3:]
    small_unit = (step, width)
    units = [small_unit if k % 4 == 3 else unit for k in range(4 * layers)]
    count = len(units)
    whole = (layers, PLANE, depth, 2, -1, tokens)
    kept = [
        array.reshape(whole) if array.ndim == 3 and array.shape[1] == 4 * width else array
        for array in saved
    ]
    scratch = [pltpu.VMEM(array.shape[1:], array.dtype) for array in kept]
    scratch += [pltpu.VMEM(*shapes[name]) for name in BACK_SCRATCH]
    scratch += [
        pltpu.VMEM((4, PLANE, depth) + unit, low),
        pltpu.VMEM((layers, PLANE, depth) + small_unit, low),
    ]
    fill = 1
    landing = [((2, depth // 2) + one, (2, depth) + one, (depth + 1, 1) + one) for one in units]
    landing[fill] = (
        (2, unit[0] // 2, width),
        (2,) + unit,
        (depth + 1, PLANE) + unit,
    )
    for n in range(3):
        scratch += [pltpu.VMEM(shapes_of[n], low) for shapes_of in landing]
    scratch += [pltpu.VMEM(one, full) for one in units]
    scratch += [
        dma((len(gathered),)),
        dma((len(SAVED), layers)),
        dma((count,)),
        dma((layers, LINKS)),
        dma((layers, LINKS)),
        dma((count, 6)),
        dma((count, 6)),
        dma((count + 3, 2, depth)),
        dma((count + 3, 2, depth)),
    ]
    scratch += AllSum.scratch(vectors.shape)
    results = pl.pallas_call(
        functools.partial(backward_kernel, depth, layers, narrow, span, step),
        out_shape=[jax.ShapeDtypeStruct(one, full) for one in units]
        + [
            jax.ShapeDtypeStruct(vectors.shape, full),
            jax.ShapeDtypeStruct((tokens, width), full),
            jax.ShapeDtypeStruct((narrow, tokens), full),
        ],
        in_specs=[ANY] * (len(gathered) + len(kept)) + [IN_VMEM] * 4,
        out_specs=[ANY] * count + [IN_VMEM] * 3,
        scratch_shapes=scratch,
        compiler_params=pltpu.CompilerParams(
            collective_id=1, has_side_effects=True, vmem_limit_bytes=67000000
        ),
        name="backward_blocks",
    )(*gathered, *kept, vectors, text_cot, layout_cot, onehot)
    return results


def finish_kernel(depth, layers, narrow, span, small_span, *refs):
    count = 4 * layers
    summed, totals, ins = refs[:count], refs[count], refs[count + 1 : count + 5]
    outs = refs[count + 5 :]
    width = ins[0].shape[1]
    at, unused = place(depth)
    for n in range(4):
        outs[n][...] = ins[n][...]
    attn, up, down = outs[4:7]
    pieces = outs[7:9] + outs[12:13]
    small_attn, small_up, small_down = outs[9:12]
    for layer in range(layers):
        parts = summed[4 * (layers - 1 - layer) :]
        down[layer] = parts[0][...]
        up[layer] = parts[1][...]
        attn[layer] = parts[2][...]
        small = parts[3]
        small_attn[layer] = small[0:small_span, 0:narrow]
        small_up[layer] = small[0:small_span, PAD : PAD + narrow]
        small_down[layer] = small[0:small_span, 2 * PAD : 2 * PAD + narrow]
    lane = lane_of((layers, width))
    found = [jnp.zeros((layers, width), jnp.float32) for piece in pieces]
    for row, n, base, lanes in flat_rows(width, narrow):
        first = at.me * pieces[n].shape[1] - base
        rows = jnp.concatenate(
            [totals[pl.ds(layer * VECTOR_ROWS + row, 1), :] for layer in range(layers)], axis=0
        )
        rolled = pltpu.roll(rows, lax.rem(16 * width - first, width), 1)
        index = lane + first
        found[n] = found[n] + jnp.where((index >= 0) & (index < lanes), rolled, 0.0)
    for n, piece in enumerate(pieces):
        piece[...] = found[n][:, : piece.shape[1]]


def run_finish(depth, layers, narrow, span, small_span, lengths, results, text_out, layout_out):
    count = 4 * layers
    summed, (totals, text_grad, layout_grad) = results[:count], results[count:]
    tokens, width = text_out.shape
    shapes = [
        (tokens, width),
        (narrow, tokens),
        (tokens, width),
        (narrow, tokens),
        (layers, span, width),
        (layers, span, width),
        (layers, span, width),
        (layers, lengths[0]),
        (layers, lengths[1]),
        (layers, small_span, narrow),
        (layers, small_span, narrow),
        (layers, small_span, narrow),
        (layers, lengths[2]),
    ]
    return pl.pallas_call(
        functools.partial(finish_kernel, depth, layers, narrow, span, small_span),
        out_shape=[jax.ShapeDtypeStruct(shape, jnp.float32) for shape in shapes],
        in_specs=[IN_VMEM] * (count + 5),
        out_specs=[IN_VMEM] * len(shapes),
        name="finish",
    )(*summed, totals, text_out, layout_out, text_grad, layout_grad)


def block_shards(
    depth,
    text_input,
    layout_input,
    text_cot,
    layout_cot,
    segment_ids,
    page_groups,
    lang_table,
    text_attn,
    text_up,
    text_down,
    text_vector,
    layout_attn,
    layout_up,
    layout_down,
    layout_vector,
):
    layers, unused, span = text_attn.shape
    narrow, small_span = layout_input.shape[1], layout_down.shape[1]
    step = PAD * PLANE // (PLANE * depth * 2)

    def turned(array):
        return jnp.swapaxes(array, -1, -2)

    weights = (
        turned(text_attn),
        turned(text_up),
        text_down,
        turned(layout_attn),
        turned(layout_up),
        layout_down,
    )
    pieces = (text_vector, lang_table, layout_vector)
    gathered, (vectors, onehot, text_out, layout_out), saved = run_forward(
        depth,
        narrow,
        step,
        weights,
        pieces,
        text_input,
        turned(layout_input),
        segment_ids.reshape(1, -1),
        page_groups.reshape(1, -1),
    )
    text_gathered = [part for n, part in enumerate(gathered) if n != 1]
    results = run_backward(
        depth,
        layers,
        narrow,
        small_span,
        step,
        text_gathered,
        saved,
        vectors,
        text_cot,
        turned(layout_cot),
        onehot,
    )
    lengths = [piece.shape[1] for piece in pieces]
    outs = run_finish(
        depth, layers, narrow, span, small_span, lengths, results, text_out, layout_out
    )
    return tuple(turned(out) if n in (1, 3, 4, 5, 9, 10) else out for n, out in enumerate(outs))


def solution(mesh):
    in_specs = (
        P(AXES, None),
        P(AXES, None),
        P(AXES, None),
        P(AXES, None),
        P(AXES),
        P(AXES),
        P(None, AXES),
        P(None, None, AXES),
        P(None, None, AXES),
        P(None, AXES, None),
        P(None, AXES),
        P(None, None, AXES),
        P(None, None, AXES),
        P(None, AXES, None),
        P(None, AXES),
    )
    out_specs = (
        P(AXES, None),
        P(AXES, None),
        P(AXES, None),
        P(AXES, None),
        P(None, None, AXES),
        P(None, None, AXES),
        P(None, AXES, None),
        P(None, AXES),
        P(None, AXES),
        P(None, None, AXES),
        P(None, None, AXES),
        P(None, AXES, None),
        P(None, AXES),
    )
    plan = functools.partial(block_shards, mesh.shape[AXES[1]] // 2) if fits_blocks(mesh) else generic_shards
    return jax.shard_map(plan, mesh=mesh, in_specs=in_specs, out_specs=out_specs, check_vma=False)
```

profile of v0, /device:TPU:0, one launch (start us, length us, event | category | flops | bytes accessed | tf_op | source)
XLA Modules:
  0.0 284.3 jit_solution(18129586018662087266)
XLA Ops:
  0.6 139.7 %forward_blocks.1 = (bf16[4,4,2,96,768]{4,3,2,1,0:T(8,128)(2,1)}, bf16[4,4,2,64,768]{4,3,2,1,0:T(8,128)(2,1)}, bf16[4,4,2,96,768]{4,3,2,1,0:T(8,128)(2,1)}, bf16...) custom-call(bf16[2,96,768]{2,1,0:T(8,128)(2,1)} %bitcast.16, ...), custom_call_target="tpu_custom_call" | custom-call | tf_op jit(solution)/shard_map/forward_blocks/pallas_call | solution.py:1297
  140.4 140.1 %backward_blocks.1 = (f32[96,768]{1,0:T(8,128)}, f32[96,768]{1,0:T(8,128)}, f32[96,768]{1,0:T(8,128)}, f32[32,768]{1,0:T(8,128)}, f32[96,768]{1,0:T(8,128)}, /*i...) custom-call(bf16[4,4,2,96,768]{4,3,2,1,0:T(8,128)(2,1)} %get-tuple-e, ...), custom_call_target="tpu_custom_call" | custom-call | tf_op jit(solution)/shard_map/backward_blocks/pallas_call | solution.py:2056
  280.4 3.7 %finish.1 = (f32[128,768]{1,0:T(8,128)}, f32[192,128]{1,0:T(8,128)}, f32[128,768]{1,0:T(8,128)}, f32[192,128]{1,0:T(8,128)}, f32[2,96,768]{2,1,0:T(8,128)}, /*in...) custom-call(f32[96,768]{1,0:T(8,128)} %get-tuple-element.83.refs_0_,, ...), custom_call_target="tpu_custom_call" | custom-call | tf_op jit(solution)/shard_map/finish/pallas_call | solution.py:2128
where the time goes:
time: 285 us; the launch traced here: 284 us
  Pallas kernels  283 us (99%)
    pallas_call x1, Pallas kernels, run_backward(): pl.pallas_call(functools.partial(backward_kernel, depth, layers, narrow,...  140 us
    pallas_call x1, Pallas kernels, run_forward(): pl.pallas_call(functools.partial(forward_kernel, depth, layers, narrow, s...  140 us

commit v1 on v0

--- a/solution.py
+++ b/solution.py
@@ -546,7 +546,7 @@
 
 
 class Plan:
-    LAG = dict(x=1.8, z=1.8, c=1.0, h=0.3)
+    LAG = dict(x=2.4, z=2.4, c=1.0, h=0.3)
     PATIENCE = 1.0
 
     def __init__(self):
@@ -650,14 +650,21 @@
     return upper * cdf, cdf + upper * density
 
 
-def natural_rows(span, step):
-    row = lax.broadcasted_iota(jnp.int32, (PAD, PAD), 0)
-    column = lax.broadcasted_iota(jnp.int32, (PAD, PAD), 1)
-    unit = jnp.zeros((PAD, PAD), jnp.int32)
-    for n in range(1, PAD // step):
-        unit = unit + jnp.where(row >= n * span, 1, 0)
-    source = unit * step + row - unit * span
-    return jnp.where((source == column) & (row < (PAD // step) * span), 1.0, 0.0)
+def unit_of(index, size, count):
+    unit = jnp.zeros(index.shape, jnp.int32)
+    for n in range(1, count):
+        unit = unit + jnp.where(index >= n * size, 1, 0)
+    return unit
+
+
+def natural_rows(span, layers, layer):
+    units = 8
+    shape = (PAD, units * layers * span)
+    row = lax.broadcasted_iota(jnp.int32, shape, 0)
+    column = lax.broadcasted_iota(jnp.int32, shape, 1)
+    unit = unit_of(row, span, units)
+    source = unit * (layers - 1) * span + layer * span + row
+    return jnp.where((source == column) & (row < units * span), 1.0, 0.0)
 
 
 def saved_shapes(layers, tokens, width, narrow_hidden):
@@ -708,14 +715,11 @@
         lax.fori_loop(0, 3, body, 0)
 
     def prepare_small():
-        permute = natural_rows(span, m.small_raw.shape[3] // m.small_raw_layers).astype(low)
-        step = m.small_raw.shape[3] // m.small_raw_layers
+        permute = natural_rows(span, m.small_raw_layers, layer).astype(low)
 
         def body(block, carry):
             for member in range(3):
-                raw = m.small_raw[
-                    block, :, :, pl.ds(layer * step, step), pl.ds(member * PAD, PAD)
-                ].reshape(PAD, PAD)
+                raw = m.small_raw[block, :, :, :, pl.ds(member * PAD, PAD)].reshape(-1, PAD)
                 rows = dot_nn(permute, raw).astype(low)
                 if member == 0:
                     m.small_attn[layer, block] = rows
@@ -858,7 +862,7 @@
     return after_attn, after_small, after_up, after_down
 
 
-def forward_shapes(layers, depth, tokens, width, narrow, step):
+def forward_shapes(layers, depth, tokens, width, narrow, small_span):
     low, full = jnp.bfloat16, jnp.float32
     span = 4 * width // (PLANE * depth * 2)
     whole = (PLANE, depth, 2, span, width)
@@ -866,9 +870,9 @@
         attn_w=(whole, low),
         up_w=(whole, low),
         down_w=(whole, low),
-        small_raw=((PLANE, depth, 2, layers * step, width), low),
-        own_small=((layers * step, width), low),
-        own_small_full=((layers * step, width), full),
+        small_raw=((PLANE, depth, 2, layers * small_span, width), low),
+        own_small=((layers * small_span, width), low),
+        own_small_full=((layers * small_span, width), full),
         same=((tokens, tokens), full),
         x=((tokens, width), full),
         y=((tokens, PAD), full),
@@ -920,7 +924,6 @@
     half = depth // 2
     low, full = jnp.bfloat16, jnp.float32
     tokens, width = m.x.shape
-    step = m.own_small.shape[0] // layers
     vectors = AllSum(devices, vector_out, *all_sum)
 
     sources = [text_attn.at[0], m.own_small]
@@ -1068,7 +1071,7 @@
         m.own_small_full[...] = jnp.zeros_like(m.own_small_full)
         units = layout_down.shape[1]
         for layer in range(layers):
-            rows = pl.ds(layer * step, units)
+            rows = pl.ds(layer * units, units)
             m.own_small_full[rows, 0:narrow] = layout_attn[layer].astype(full)
             m.own_small_full[rows, PAD : PAD + narrow] = layout_up[layer].astype(full)
             m.own_small_full[rows, 2 * PAD : 2 * PAD + narrow] = layout_down[layer].astype(full)
@@ -1284,15 +1287,16 @@
                         line(k, rising, hop, side).wait_send()
 
 
-def run_forward(depth, narrow, step, weights, pieces, text_in, layout_in, page_row, groups):
+def run_forward(depth, narrow, weights, pieces, text_in, layout_in, page_row, groups):
     dma = pltpu.SemaphoreType.DMA
     tokens, width = text_in.shape
     layers, span, unused = weights[0].shape
     count = 3 * layers + 1
     full = jnp.float32
     saved = saved_shapes(layers, tokens, width, 4 * narrow)
-    scratch = forward_shapes(layers, depth, tokens, width, narrow, step)
-    rows = [span, layers * step] + [span] * (count - 2)
+    small_span = weights[5].shape[1]
+    scratch = forward_shapes(layers, depth, tokens, width, narrow, small_span)
+    rows = [span, layers * small_span] + [span] * (count - 2)
     vector_shape = (layers * VECTOR_ROWS, width)
     results = pl.pallas_call(
         functools.partial(forward_kernel, depth, layers, narrow, span),
@@ -1384,20 +1388,17 @@
     return jnp.sum(rows.astype(jnp.float32), axis=0, keepdims=True)
 
 
-def padded_rows_of_core(span, step, core):
-    units = PAD // step // 2
-    shape = (units * step, units * 2 * span)
+def rows_of_core(span, layers, layer, depth, core):
+    shape = (depth * layers * span, 2 * depth * span)
     row = lax.broadcasted_iota(jnp.int32, shape, 0)
     column = lax.broadcasted_iota(jnp.int32, shape, 1)
-    unit = jnp.zeros(shape, jnp.int32)
-    for n in range(1, units):
-        unit = unit + jnp.where(row >= n * step, 1, 0)
-    inside = row - unit * step
+    unit = unit_of(row, layers * span, depth)
+    inside = row - unit * layers * span - layer * span
     source = (2 * unit + core) * span + inside
-    return jnp.where((source == column) & (inside < span), 1.0, 0.0)
-
-
-def backward_kernel(depth, layers, narrow, span, step, *refs):
+    return jnp.where((source == column) & (inside >= 0) & (inside < span), 1.0, 0.0)
+
+
+def backward_kernel(depth, layers, narrow, span, *refs):
     refs = list(refs)
 
     def take(number):
@@ -1406,12 +1407,14 @@
         return taken
 
     text_count = TEXT_MEMBERS * layers
-    count = (TEXT_MEMBERS + 1) * layers
+    count = text_count + 1
     gathered = take(text_count)
     kept = take(len(SAVED))
     vec_ref, text_cot, layout_cot, onehot = take(4)
     finals = take(count)
     vector_out, text_out, layout_out = take(3)
+    layout_turned, early_sem = refs[-2:]
+    del refs[-2:]
     m = SimpleNamespace()
     for name in SAVED + BACK_SCRATCH:
         setattr(m, name, refs.pop(0))
@@ -1429,12 +1432,11 @@
     tokens, width = m.gx.shape
     hidden_small = m.upper_low_small.shape[1]
     signal(devices)
-    greeted()
     vectors = AllSum(devices, vector_out, *all_sum)
 
     slots, reuse = {}, {}
     for k in range(count):
-        if k % 4 != 3:
+        if k < text_count:
             spare = [n for n in range(mine_text.shape[0]) if n not in slots.values()]
             if spare:
                 slots[k] = spare[0]
@@ -1443,8 +1445,8 @@
                 slots[k] = slots[reuse[k]]
 
     def mine(k):
-        if k % 4 == 3:
-            return mine_small.at[k // 4]
+        if k == text_count:
+            return mine_small
         return mine_text.at[slots[k]]
 
     order = []
@@ -1571,6 +1573,12 @@
 
         if k != fill:
             put_out(k).start()
+
+    def early():
+        return (
+            pltpu.make_async_copy(m.gx, text_out, early_sem.at[0]),
+            pltpu.make_async_copy(layout_turned, layout_out, early_sem.at[1]),
+        )
 
     def put_out(k):
         return pltpu.make_async_copy(outs[k], finals[k], out_sem.at[k])
@@ -1682,9 +1690,10 @@
     for name in names:
         saved_load(name, layers - 1).start()
     weight_load(1).start()
+    greeted()
 
     def add_layer(turn, layer):
-        k = 4 * turn
+        k = TEXT_MEMBERS * turn
         vec = lambda row, n=1: vec_ref[pl.ds(layer * VECTOR_ROWS + row, n), :]
         small_vec = lambda row: vec(SMALL_ROW + row)[:, :PAD]
         slot = lambda member: m.weights.at[(3 * turn + member) % 2]
@@ -1928,15 +1937,16 @@
             for group in range(LANGS):
                 put(TABLE_ROW + group, total(onehot[:, group : group + 1] * m.gx[...]))
             if layer == 0:
-                text_out[...] = m.gx[...]
-                layout_out[...] = m.gy[:, 0:narrow].T
+                layout_turned[...] = m.gy[:, 0:narrow].T
+                for one in early():
+                    one.start()
                 vector_out[...] = m.sums[...]
                 vectors.send(0)
 
         def small_sums():
             for link in (5, 6, 7, 8, 9):
                 cross(layer, link).wait_recv()
-            arrange = padded_rows_of_core(span, step, core).astype(low)
+            arrange = rows_of_core(span, layers, layer, depth, core).astype(low)
             small_rows = (m.rows_small.at[1], m.rows_small.at[0], m.turned_small)
             small_land = (2, 1, 0)
             for member in range(3):
@@ -1953,16 +1963,19 @@
                     )
                     right = jnp.concatenate([own_in, m.in_land_small[layer, source]], axis=0)
                     placed = dot_nn(arrange, dot_nn(left, right).astype(low)).astype(low)
-                    mine(k + 3)[block, :, :, pl.ds(member * PAD, PAD)] = placed.reshape(
-                        depth, step, PAD
-                    )
+                    placed = placed.reshape(depth, layers * span, PAD)
+                    lanes = pl.ds(member * PAD, PAD)
+                    if turn > 0:
+                        placed = mine_small[block, :, :, lanes] + placed
+                    mine_small[block, :, :, lanes] = placed
             if layer > 0:
                 for link in range(LINKS):
                     cross(layer, link).wait_send()
                 for name in names:
                     saved_load(name, layer - 1).start()
-            for index in range(4):
-                plane(k + 3, index).start()
+            if layer == 0:
+                for index in range(4):
+                    plane(text_count, index).start()
 
         own = lambda n: ("o", k + n)
         crossed = lambda link: ("c", layer, link)
@@ -1970,7 +1983,7 @@
         then(("t", 0, turn), tail, 1.7, sends=[("c", 1.0, crossed(1)), ("c", 0.5, crossed(2))])
         then(("t", 1, turn), tail_small, 0.2, sends=[("c", 0.8, crossed(6))])
         then(own(0), own_down, 1.4, [crossed(1), crossed(2)], own_sends(k), free(0))
-        add_scatter(k, 4 * k)
+        add_scatter(k, k)
         then(
             ("h", 0, turn), functools.partial(hidden_blocks, 0, 2), 1.4, sends=[("c", 1.5, crossed(0))]
         )
@@ -1979,7 +1992,7 @@
         )
         then(("h", 2, turn), hide_small, 0.4, sends=[("c", 0.5, crossed(8))])
         then(own(1), own_up, 1.4, [crossed(0), crossed(3)], own_sends(k + 1), free(1))
-        add_scatter(k + 1, 4 * k + 4)
+        add_scatter(k + 1, k + 1)
         then(("n", 0, turn), lower_text, 1.7)
         then(("n", 1, turn), lower_small, 0.4)
         then(("n", 2, turn), contexts, 0.4)
@@ -1987,11 +2000,14 @@
         then(("p", 1, turn), functools.partial(pairs, H // 4, H // 4), 2.7)
         then(("r", turn), turn_rows, 0.4, sends=[("c", 1.0, crossed(4)), ("c", 0.5, crossed(9))])
         then(own(2), attn_sums, 1.4, [crossed(4)], own_sends(k + 2), free(2))
-        add_scatter(k + 2, 4 * k + 8)
+        add_scatter(k + 2, k + 2)
         then(("e", turn), enter, 1.4, sends=[("c", 0.3, ("v", 0))] if layer == 0 else [])
-        late = [("s", 2, k + 2)] if layer == 0 else []
-        then(own(3), small_sums, 2.6, [crossed(9)], own_sends(k + 3), late)
-        add_scatter(k + 3, 4 * k + 12)
+        if layer > 0:
+            then(("w", turn), small_sums, 2.6, [crossed(9)])
+        else:
+            late = [("s", 2, k + 2)]
+            then(("o", text_count), small_sums, 2.6, [crossed(9)], own_sends(text_count), late)
+            add_scatter(text_count, text_count)
 
     for turn, layer in enumerate(reversed(range(layers))):
         add_layer(turn, layer)
@@ -2006,19 +2022,21 @@
     drained = list(reuse.values())
     for k in range(count):
         put_out(k).wait()
+    for one in early():
+        one.wait()
     for k in range(count):
         if k not in drained:
             drain(k)
 
 
-def run_backward(depth, layers, narrow, span, step, gathered, saved, vectors, text_cot, layout_cot, onehot):
+def run_backward(depth, layers, narrow, span, gathered, saved, vectors, text_cot, layout_cot, onehot):
     dma = pltpu.SemaphoreType.DMA
     tokens, width = text_cot.shape
     low, full = jnp.bfloat16, jnp.float32
     shapes = back_shapes(layers, depth, tokens, width, 4 * narrow)
     unit = gathered[0].shape[3:]
-    small_unit = (step, width)
-    units = [small_unit if k % 4 == 3 else unit for k in range(4 * layers)]
+    small_unit = (layers * span, width)
+    units = [unit] * (TEXT_MEMBERS * layers) + [small_unit]
     count = len(units)
     whole = (layers, PLANE, depth, 2, -1, tokens)
     kept = [
@@ -2029,7 +2047,7 @@
     scratch += [pltpu.VMEM(*shapes[name]) for name in BACK_SCRATCH]
     scratch += [
         pltpu.VMEM((4, PLANE, depth) + unit, low),
-        pltpu.VMEM((layers, PLANE, depth) + small_unit, low),
+        pltpu.VMEM((PLANE, depth) + small_unit, low),
     ]
     fill = 1
     landing = [((2, depth // 2) + one, (2, depth) + one, (depth + 1, 1) + one) for one in units]
@@ -2053,8 +2071,9 @@
         dma((count + 3, 2, depth)),
     ]
     scratch += AllSum.scratch(vectors.shape)
+    scratch += [pltpu.VMEM((narrow, tokens), full), dma((2,))]
     results = pl.pallas_call(
-        functools.partial(backward_kernel, depth, layers, narrow, span, step),
+        functools.partial(backward_kernel, depth, layers, narrow, span),
         out_shape=[jax.ShapeDtypeStruct(one, full) for one in units]
         + [
             jax.ShapeDtypeStruct(vectors.shape, full),
@@ -2062,7 +2081,7 @@
             jax.ShapeDtypeStruct((narrow, tokens), full),
         ],
         in_specs=[ANY] * (len(gathered) + len(kept)) + [IN_VMEM] * 4,
-        out_specs=[ANY] * count + [IN_VMEM] * 3,
+        out_specs=[ANY] * count + [IN_VMEM, ANY, ANY],
         scratch_shapes=scratch,
         compiler_params=pltpu.CompilerParams(
             collective_id=1, has_side_effects=True, vmem_limit_bytes=67000000
@@ -2073,7 +2092,7 @@
 
 
 def finish_kernel(depth, layers, narrow, span, small_span, *refs):
-    count = 4 * layers
+    count = TEXT_MEMBERS * layers + 1
     summed, totals, ins = refs[:count], refs[count], refs[count + 1 : count + 5]
     outs = refs[count + 5 :]
     width = ins[0].shape[1]
@@ -2084,14 +2103,14 @@
     pieces = outs[7:9] + outs[12:13]
     small_attn, small_up, small_down = outs[9:12]
     for layer in range(layers):
-        parts = summed[4 * (layers - 1 - layer) :]
+        parts = summed[TEXT_MEMBERS * (layers - 1 - layer) :]
         down[layer] = parts[0][...]
         up[layer] = parts[1][...]
         attn[layer] = parts[2][...]
-        small = parts[3]
-        small_attn[layer] = small[0:small_span, 0:narrow]
-        small_up[layer] = small[0:small_span, PAD : PAD + narrow]
-        small_down[layer] = small[0:small_span, 2 * PAD : 2 * PAD + narrow]
+        rows = summed[count - 1][layer * small_span : (layer + 1) * small_span, :]
+        small_attn[layer] = rows[:, 0:narrow]
+        small_up[layer] = rows[:, PAD : PAD + narrow]
+        small_down[layer] = rows[:, 2 * PAD : 2 * PAD + narrow]
     lane = lane_of((layers, width))
     found = [jnp.zeros((layers, width), jnp.float32) for piece in pieces]
     for row, n, base, lanes in flat_rows(width, narrow):
@@ -2107,7 +2126,7 @@
 
 
 def run_finish(depth, layers, narrow, span, small_span, lengths, results, text_out, layout_out):
-    count = 4 * layers
+    count = TEXT_MEMBERS * layers + 1
     summed, (totals, text_grad, layout_grad) = results[:count], results[count:]
     tokens, width = text_out.shape
     shapes = [
@@ -2154,7 +2173,6 @@
 ):
     layers, unused, span = text_attn.shape
     narrow, small_span = layout_input.shape[1], layout_down.shape[1]
-    step = PAD * PLANE // (PLANE * depth * 2)
 
     def turned(array):
         return jnp.swapaxes(array, -1, -2)
@@ -2171,7 +2189,6 @@
     gathered, (vectors, onehot, text_out, layout_out), saved = run_forward(
         depth,
         narrow,
-        step,
         weights,
         pieces,
         text_input,
@@ -2185,7 +2202,6 @@
         layers,
         narrow,
         small_span,
-        step,
         text_gathered,
         saved,
         vectors,

time: 285 us -> 279 us (0.979)
  Pallas kernels: 283 us -> 277 us
    pallas_call x1, Pallas kernels: 140 us -> 136 us  [run_backward(): pl.pallas_call(functools.partial(backward_kernel, depth, layers, narrow,...]
where the time goes in v1:
time: 279 us; the launch traced here: 278 us
  Pallas kernels  277 us (99%)
    pallas_call x1, Pallas kernels, run_forward(): pl.pallas_call(functools.partial(forward_kernel, depth, layers, narrow, s...  138 us
    pallas_call x1, Pallas kernels, run_backward(): pl.pallas_call(functools.partial(backward_kernel, depth, layers, narrow,...  136 us

profile of v1, /device:TPU:0, one launch (start us, length us, event | category | flops | bytes accessed | tf_op | source)
XLA Modules:
  0.0 278.3 jit_solution(554123771350571469)
XLA Ops:
  0.6 138.2 %forward_blocks.1 = (bf16[4,4,2,96,768]{4,3,2,1,0:T(8,128)(2,1)}, bf16[4,4,2,48,768]{4,3,2,1,0:T(8,128)(2,1)}, bf16[4,4,2,96,768]{4,3,2,1,0:T(8,128)(2,1)}, bf16...) custom-call(bf16[2,96,768]{2,1,0:T(8,128)(2,1)} %bitcast.16, ...), custom_call_target="tpu_custom_call" | custom-call | tf_op jit(solution)/shard_map/forward_blocks/pallas_call | solution.py:1301
  138.8 135.6 %backward_blocks.1 = (f32[96,768]{1,0:T(8,128)}, f32[96,768]{1,0:T(8,128)}, f32[96,768]{1,0:T(8,128)}, f32[96,768]{1,0:T(8,128)}, f32[96,768]{1,0:T(8,128)}, /*i...) custom-call(bf16[4,4,2,96,768]{4,3,2,1,0:T(8,128)(2,1)} %get-tuple-eleme, ...), custom_call_target="tpu_custom_call" | custom-call | tf_op jit(solution)/shard_map/backward_blocks/pallas_call | solution.py:2075
  274.5 3.6 %finish.1 = (f32[128,768]{1,0:T(8,128)}, f32[192,128]{1,0:T(8,128)}, f32[128,768]{1,0:T(8,128)}, f32[192,128]{1,0:T(8,128)}, f32[2,96,768]{2,1,0:T(8,128)}, /*in...) custom-call(f32[96,768]{1,0:T(8,128)} %get-tuple-element.82.refs_0_,, ...), custom_call_target="tpu_custom_call" | custom-call | tf_op jit(solution)/shard_map/finish/pallas_call | solution.py:2147

commit v2 on v1

--- a/solution.py
+++ b/solution.py
@@ -1236,7 +1236,7 @@
     vector_steps = [spread_vectors]
     vector_steps += [functools.partial(vectors.advance, n) for n in range(AllSum.STEPS)]
     for n, step_of in enumerate(vector_steps):
-        link, amount = (("c", 0.3), ("z", 2.2), ("z", 6.0), ("x", 2.2), ("x", 2.2), ("h", 0.0))[n]
+        link, amount = (("c", 0.3), ("z", 2.2), ("z", 4.0), ("x", 2.2), ("x", 2.2), ("h", 0.0))[n]
         sends = [(link, amount, ("v", n))]
         needs = [("v", n - 1)] if n else []
         after = [("v", n - 1)] if n else []
@@ -1631,13 +1631,17 @@
             first, share = ("f", 0), one / 2
             sends = [("x", share, ("d", k)), ("x", share, ("e", k))]
             ends = [("z", depth - 1, k, side) for side in range(PLANE)]
+            ends.append(("s", 2, text_count))
             plan.add(first, fill_plane, ends, [], sends, 0.2, rank)
         plan.add(
             ("s", 2, k), functools.partial(second_sums, k), [first], [("d", k)], [("x", share, ("g", k))], 0.5, rank
         )
         sends = [(("z", 0), (depth - 1) * one, ("z", 1, k, 0))] if k != fill else []
+        before = [("s", 2, k)]
+        if k == fill:
+            before.append(("z", 1, text_count - 1, 0))
         plan.add(
-            ("s", 3, k), functools.partial(third_sums, k), [("s", 2, k)], [("e", k), ("g", k)], sends, 1.0, rank
+            ("s", 3, k), functools.partial(third_sums, k), before, [("e", k), ("g", k)], sends, 1.0, rank
         )
 
     def own_sends(k):
@@ -2014,6 +2018,8 @@
     for n in range(AllSum.STEPS):
         sends = [((("z", 0), 2.2), (("z", 0), 4.4), ("x", 2.2), ("x", 2.2), ("c", 0.0))[n] + (("v", n + 1),)]
         after = [("v", n - 1)] if n else [("e", layers - 1)]
+        if n == 3:
+            after.append(("z", 1, text_count - 1, 0))
         plan.add(("v", n), functools.partial(vectors.advance, n), after, [("v", n)], sends, 0.2, -1)
     plan.run()
     vectors.close()

time: 279 us -> 270 us (0.968)
  Pallas kernels: 277 us -> 269 us
    pallas_call x1, Pallas kernels: 138 us -> 133 us  [run_forward(): pl.pallas_call(functools.partial(forward_kernel, depth, layers, narrow, s...]
where the time goes in v2:
time: 270 us
  Pallas kernels  269 us (100%)
    pallas_call x1, Pallas kernels, run_backward(): pl.pallas_call(functools.partial(backward_kernel, depth, layers, narrow,...  133 us
    pallas_call x1, Pallas kernels, run_forward(): pl.pallas_call(functools.partial(forward_kernel, depth, layers, narrow, s...  133 us

profile of v2, /device:TPU:0, one launch (start us, length us, event | category | flops | bytes accessed | tf_op | source)
XLA Modules:
  0.0 270.1 jit_solution(618976876508000641)
XLA Ops:
  0.6 132.8 %forward_blocks.1 = (bf16[4,4,2,96,768]{4,3,2,1,0:T(8,128)(2,1)}, bf16[4,4,2,48,768]{4,3,2,1,0:T(8,128)(2,1)}, bf16[4,4,2,96,768]{4,3,2,1,0:T(8,128)(2,1)}, bf16...) custom-call(bf16[2,96,768]{2,1,0:T(8,128)(2,1)} %bitcast.16, ...), custom_call_target="tpu_custom_call" | custom-call | tf_op jit(solution)/shard_map/forward_blocks/pallas_call | solution.py:1301
  133.5 132.9 %backward_blocks.1 = (f32[96,768]{1,0:T(8,128)}, f32[96,768]{1,0:T(8,128)}, f32[96,768]{1,0:T(8,128)}, f32[96,768]{1,0:T(8,128)}, f32[96,768]{1,0:T(8,128)}, /*i...) custom-call(bf16[4,4,2,96,768]{4,3,2,1,0:T(8,128)(2,1)} %get-tuple-eleme, ...), custom_call_target="tpu_custom_call" | custom-call | tf_op jit(solution)/shard_map/backward_blocks/pallas_call | solution.py:2081
  266.3 3.6 %finish.1 = (f32[128,768]{1,0:T(8,128)}, f32[192,128]{1,0:T(8,128)}, f32[128,768]{1,0:T(8,128)}, f32[192,128]{1,0:T(8,128)}, f32[2,96,768]{2,1,0:T(8,128)}, /*in...) custom-call(f32[96,768]{1,0:T(8,128)} %get-tuple-element.82.refs_0_,, ...), custom_call_target="tpu_custom_call" | custom-call | tf_op jit(solution)/shard_map/finish/pallas_call | solution.py:2153
